TPU v7x, 64 devices: a 2x2x8 block of a 4x4x8 slice. The times are simulated.
64 devices in a mesh: dp: 4 (over x, y), cp: 16 (over z, core).
Axes of the slice: x: 2, y: 2, z: 8, core: 2. Of those that a mesh axis runs over, the one named last changes fastest.
The devices are a block of a 4x4x8 slice.
Arguments:
- x_tok: bfloat16 [128, 5120], P(('dp', 'cp')), parts along dimension 0
- prompt_lens: int32 [128], P('dp'), parts along dimension 0
- k_cache: bfloat16 [128, 1024, 8, 128], P('dp', 'cp'), parts along dimension 0
- v_cache: bfloat16 [128, 1024, 8, 128], P('dp', 'cp'), parts along dimension 0
- norm_gain: bfloat16 [5120], replicated
- w_q: bfloat16 [5120, 5120], replicated
- b_q: bfloat16 [5120], replicated
- w_k: bfloat16 [5120, 1024], replicated
- b_k: bfloat16 [1024], replicated
- w_v: bfloat16 [5120, 1024], replicated
- b_v: bfloat16 [1024], replicated
- w_o: bfloat16 [5120, 5120], replicated
Outputs:
- output 1: bfloat16 [128, 5120], P(('dp', 'cp')), parts along dimension 0
- output 2: bfloat16 [128, 1024, 8, 128], P(('dp', 'cp')), parts along dimension 0
- output 3: bfloat16 [128, 1024, 8, 128], P(('dp', 'cp')), parts along dimension 0
There are 4 independent parts. A program takes and returns all parts, laid end to end along the dimension named above; an argument that names none is the same for every part.
All inputs are finite; a program needn't handle non-finite values.
Results may differ from a plain program's by a relative error of at most 0.00629694.
Values are sent between devices in bfloat16 or wider.
A program may use at most 768 MiB of HBM per device.

v0:
```python
import jax
import jax.numpy as jnp
from jax import lax
from jax.sharding import PartitionSpec as P

RMS_EPS = 1e-6
ROPE_THETA = 1000000.0


def rotary(vectors, positions):
    head_dim = vectors.shape[-1]
    half_dim = head_dim // 2
    inv_freq = jnp.power(ROPE_THETA, -(jnp.arange(half_dim, dtype=jnp.float32) * 2.0 / head_dim))
    angle = positions.astype(jnp.float32)[:, None, None] * inv_freq
    cos_t = jnp.cos(angle)
    sin_t = jnp.sin(angle)
    first = vectors[..., :half_dim]
    second = vectors[..., half_dim:]
    return jnp.concatenate([first * cos_t - second * sin_t, second * cos_t + first * sin_t], axis=-1)


def project(x_tok, positions, norm_gain, w_q, b_q, w_k, b_k, w_v, b_v, head_dim):
    rows = x_tok.shape[0]
    x_wide = x_tok.astype(jnp.float32)
    mean_sq = jnp.mean(x_wide * x_wide, axis=-1, keepdims=True)
    normed = (x_wide * lax.rsqrt(mean_sq + RMS_EPS) * norm_gain.astype(jnp.float32)).astype(jnp.bfloat16)
    query = jnp.dot(normed, w_q, preferred_element_type=jnp.float32) + b_q.astype(jnp.float32)
    query = rotary(query.reshape(rows, -1, head_dim), positions).astype(jnp.bfloat16)
    key_new = jnp.dot(normed, w_k, preferred_element_type=jnp.float32) + b_k.astype(jnp.float32)
    key_new = rotary(key_new.reshape(rows, -1, head_dim), positions).astype(jnp.bfloat16)
    value_new = jnp.dot(normed, w_v, preferred_element_type=jnp.float32) + b_v.astype(jnp.float32)
    value_new = value_new.reshape(rows, -1, head_dim).astype(jnp.bfloat16)
    return query, key_new, value_new


def decode_local(x_tok, positions, keys_old, vals_old, norm_gain, w_q, b_q, w_k, b_k, w_v, b_v, w_o):
    rows, seq_len, kv_heads, head_dim = keys_old.shape
    query, key_new, value_new = project(x_tok, positions, norm_gain, w_q, b_q, w_k, b_k, w_v, b_v, head_dim)
    heads = query.shape[1]
    group = heads // kv_heads
    slot_idx = lax.broadcasted_iota(jnp.int32, (1, seq_len, 1, 1), 1)
    pos_col = positions[:, None, None, None]
    zero_val = jnp.zeros((), jnp.bfloat16)
    keys_all = jnp.where(slot_idx < pos_col, keys_old, jnp.where(slot_idx == pos_col, key_new[:, None], zero_val))
    vals_all = jnp.where(slot_idx < pos_col, vals_old, jnp.where(slot_idx == pos_col, value_new[:, None], zero_val))
    scores = jnp.einsum('bkgd,bskd->bkgs', query.reshape(rows, kv_heads, group, head_dim), keys_all, preferred_element_type=jnp.float32) * (head_dim ** -0.5)
    valid = lax.broadcasted_iota(jnp.int32, (1, 1, 1, seq_len), 3) <= pos_col
    scores = jnp.where(valid, scores, -1e30)
    row_max = jnp.max(scores, axis=-1, keepdims=True)
    weights = jnp.exp(scores - row_max)
    weight_sum = jnp.sum(weights, axis=-1, keepdims=True)
    mixed = jnp.einsum('bkgs,bskd->bkgd', weights.astype(jnp.bfloat16), vals_all, preferred_element_type=jnp.float32) / weight_sum
    attended = mixed.reshape(rows, heads * head_dim).astype(jnp.bfloat16)
    y_out = (x_tok.astype(jnp.float32) + jnp.dot(attended, w_o, preferred_element_type=jnp.float32)).astype(jnp.bfloat16)
    return y_out, keys_all, vals_all


def solution(mesh):
    batch_spec = P(('dp', 'cp'))
    seq_spec = P('dp', 'cp')
    whole = P()

    def per_device(x_tok, prompt_lens, k_cache, v_cache, norm_gain, w_q, b_q, w_k, b_k, w_v, b_v, w_o):
        rows = x_tok.shape[0]
        first_row = lax.axis_index('cp') * rows
        positions = lax.dynamic_slice_in_dim(prompt_lens, first_row, rows)
        keys_old = lax.all_to_all(k_cache, 'cp', 0, 1, tiled=True)
        vals_old = lax.all_to_all(v_cache, 'cp', 0, 1, tiled=True)
        return decode_local(x_tok, positions, keys_old, vals_old, norm_gain, w_q, b_q, w_k, b_k, w_v, b_v, w_o)

    return jax.shard_map(per_device, mesh=mesh, in_specs=(batch_spec, P('dp'), seq_spec, seq_spec, whole, whole, whole, whole, whole, whole, whole, whole), out_specs=(batch_spec, batch_spec, batch_spec), check_vma=False)
```

profile of v0, /device:TPU:53, one launch (start us, length us, event | category | flops | bytes accessed | tf_op | source)
XLA Modules:
  0.0 237.8 jit_solution(14822851703354959853)
XLA Ops:
  0.6 102.7 %all_to_all.36 = bf16[32,64,8,128]{3,2,1,0:T(8,128)(2,1)} all-to-all(bf16[32,64,8,128]{3,2,1,0:T(8,128)(2,1)} %param.14), channel_id=1, replica_groups=mesh['dp'=4,'cp'=16] {'cp'}, dimensions={0} | all-to-all | bytes 8388608 | tf_op jit(solution)/shard_map/all_to_all | solution.py:67
  103.3 0.0 copy-start.6
  103.3 0.0 copy-start.7
  103.3 0.0 copy-start.4
  103.3 0.0 copy-start.3
  103.3 0.0 slice-start
  103.4 6.7 %all-to-all-start.1 = ((bf16[32,64,8,128]{3,2,1,0:T(8,128)(2,1)}), bf16[32,64,8,128]{3,2,1,0:T(8,128)(2,1)}, u32[]{:S(2)}, u32[]{:S(2)}) async-start(bf16[32,64,8,128]{3,2,1,0:T(8,128)(2,1)} %param.15), calls=%async_computation.1 | async-start | bytes 8388608 | tf_op jit(solution)/shard_map/all_to_all | solution.py:68
  110.0 0.0 copy-done.6
  110.1 0.0 copy-done.7
  110.1 0.0 copy-done.4
  110.1 0.0 copy-done.3
  110.1 0.2 fusion.25
  110.3 0.0 slice-start.1
  110.3 0.0 slice-start.2
  110.3 5.6 %fusion.20 = bf16[1,2,8,128]{3,1,2,0:T(2,128)(2,1)S(1)} fusion(bf16[5120,1024]{1,0:T(8,128)(2,1)} %param.21, f32[1024]{0:T(1024)S(1)} %convert_element_type.59, bf16[2,5120]{1,0:T(2,128)(2,1)S(1)} %copy-done.3, f32[2]{0:T(128)S(1)} %add_rsqrt_fusion, f32[5120]{0:T(1024)S(1)} %convert_element_type.53), kind=kOutput, calls=%fused_computation.18 | convolution fusion | flops 21016576 | bytes 10534920 | tf_op jit(solution)/shard_map/dot_general | solution.py:31
  115.9 0.0 slice-done
  115.9 0.0 slice-done.1
  115.9 0.8 slice-done.2
  116.7 0.0 copy-start.5
  116.7 0.0 copy-start.8
  116.7 1.5 fusion.18
  118.2 0.0 copy-done.5
  118.3 0.0 copy-done.8
  118.3 0.1 fusion.35
  118.4 0.1 multiply_cosine_fusion
  118.5 19.5 %fusion.17 = f32[2,40,128]{2,0,1:T(2,128)S(1)} fusion(bf16[5120,5120]{1,0:T(8,128)(2,1)} %param.17, f32[5120]{0:T(1024)S(1)} %convert_element_type.55, bf16[2,5120]{1,0:T(2,128)(2,1)S(1)} %copy-done.3, f32[2]{0:T(128)S(1)} %add_rsqrt_fusion, f32[5120]{0:T(1024)S(1)} %convert_element_type.53), kind=kOutput, calls=%fused_computation.13 | convolution fusion | flops 104908800 | bytes 52531208 | tf_op jit(solution)/shard_map/dot_general | solution.py:27
  138.0 0.1 subtract_convert_fusion
  138.1 0.1 subtract_convert_fusion.1
  138.2 0.1 pad_maximum_fusion
  138.3 0.1 iota_compare_fusion.2
  138.4 4.7 %copy.23 = bf16[16,2,64,8,128]{4,3,2,0,1:T(8,128)(2,1)} copy(bf16[16,2,64,8,128]{4,3,2,1,0:T(8,128)(2,1)} %bitcast.32) | data formatting | bytes 8388608 | tf_op jit(solution)/shard_map/all_to_all | solution.py:67
  143.0 60.7 %all-to-all-done.1 = bf16[32,64,8,128]{3,2,1,0:T(8,128)(2,1)} async-done(((bf16[32,64,8,128]{3,2,1,0:T(8,128)(2,1)}), bf16[32,64,8,128]{3,2,1,0:T(8,128)(2,1)}, u32[]{:S(2)}, u32[]{:S(2)}) %all-to-all-start.1) | async-done | bytes 4194336 | tf_op jit(solution)/shard_map/all_to_all | solution.py:68
  203.7 0.0 copy-start.2
  203.7 2.6 %copy.25 = bf16[16,2,64,8,128]{4,3,2,0,1:T(8,128)(2,1)S(1)} copy(bf16[16,2,64,8,128]{4,3,2,1,0:T(8,128)(2,1)} %bitcast.7) | data formatting | bytes 8388608 | tf_op jit(solution)/shard_map/all_to_all | solution.py:68
  206.3 0.8 copy-done.2
  207.2 5.7 %select_select_fusion.1 = (bf16[2,1024,8,128]{3,2,1,0:T(8,128)(2,1)S(1)}, bf16[2,1024,8,128]{3,2,1,0:T(8,128)(2,1)S(1)}) fusion(bf16[2,1024,8,128]{3,2,1,0:T(8,128)(2,1)S(1)} %bitcast.30, pred[2,1024]{1,0:T(4,128)(4,1)S(1)} %get-tuple-element.14, pred[2,1024]{1,0:T(4,128)(4,1)S(1)} %get-tuple-element.15, bf16[2,8,128]{2,1,0:T(8,128)(2,1)S(1)} %pad_maximum_fusion, ...), kind=kLoop, calls=%fused_computation.8 | loop fusion | flops 8388608 | bytes 16789504 | tf_op jit(solution)/shard_map/jit(_where)/select_n | solution.py:44
  212.9 0.0 copy-start
  212.9 0.0 copy-start.1
  212.9 2.0 copy-done
  214.9 1.3 fusion.36
  216.2 0.2 fusion.21
  216.5 0.0 copy-done.1
  216.5 1.0 fusion.14
  217.6 20.2 %fusion = bf16[2,5120]{1,0:T(2,128)(2,1)} fusion(bf16[2,5120]{1,0:T(2,128)(2,1)S(1)} %convert_element_type.63, bf16[5120,5120]{1,0:T(8,128)(2,1)} %param.23, bf16[2,5120]{1,0:T(2,128)(2,1)S(1)} %copy-done.3), kind=kOutput, calls=%fused_computation.2 | convolution fusion | flops 104888320 | bytes 52490240 | tf_op jit(solution)/shard_map/dot_general | solution.py:54
  (12 shorter events, 0.1 us)
Async XLA Ops:
  103.3 6.7 %copy-start.6 = (bf16[1024]{0:T(1024)(128)(2,1)S(1)}, bf16[1024]{0:T(1024)(128)(2,1)}, u32[]{:S(2)}) copy-start(bf16[1024]{0:T(1024)(128)(2,1)} %param.20) | copy-start | bytes 6148
  103.3 6.7 %copy-start.7 = (bf16[1024]{0:T(1024)(128)(2,1)S(1)}, bf16[1024]{0:T(1024)(128)(2,1)}, u32[]{:S(2)}) copy-start(bf16[1024]{0:T(1024)(128)(2,1)} %param.22) | copy-start | bytes 6148
  103.3 6.7 %copy-start.4 = (bf16[5120]{0:T(1024)(128)(2,1)S(1)}, bf16[5120]{0:T(1024)(128)(2,1)}, u32[]{:S(2)}) copy-start(bf16[5120]{0:T(1024)(128)(2,1)} %param.16) | copy-start | bytes 30724
  103.3 6.8 %copy-start.3 = (bf16[2,5120]{1,0:T(2,128)(2,1)S(1)}, bf16[2,5120]{1,0:T(2,128)(2,1)}, u32[]{:S(2)}) copy-start(bf16[2,5120]{1,0:T(2,128)(2,1)} %param.12) | copy-start | bytes 61444
  103.3 12.6 %slice-start = ((s8[10485760]{0:T(1024)(128)(4,1)}), s8[2097152]{0:T(1024)(128)(4,1)S(1)}, s32[]{:S(2)}) async-start(s8[10485760]{0:T(1024)(128)(4,1)} %bitcast.28), calls=%async_computation.2 | async-start | bytes 4194304
  103.4 100.4 %all-to-all-start.1 = ((bf16[32,64,8,128]{3,2,1,0:T(8,128)(2,1)}), bf16[32,64,8,128]{3,2,1,0:T(8,128)(2,1)}, u32[]{:S(2)}, u32[]{:S(2)}) async-start(bf16[32,64,8,128]{3,2,1,0:T(8,128)(2,1)} %param.15), calls=%async_computation.1 | async-start | bytes 8388608 | tf_op jit(solution)/shard_map/all_to_all | solution.py:68
  110.3 5.7 %slice-start.1 = ((s8[10485760]{0:T(1024)(128)(4,1)}), s8[4194304]{0:T(1024)(128)(4,1)S(1)}, s32[]{:S(2)}) async-start(s8[10485760]{0:T(1024)(128)(4,1)} %bitcast.28), calls=%async_computation.3 | async-start | bytes 8388608
  110.3 6.4 %slice-start.2 = ((s8[10485760]{0:T(1024)(128)(4,1)}), s8[4194304]{0:T(1024)(128)(4,1)S(1)}, s32[]{:S(2)}) async-start(s8[10485760]{0:T(1024)(128)(4,1)} %bitcast.28), calls=%async_computation.4 | async-start | bytes 8388608
  116.7 1.5 copy-start.5
  116.7 1.5 copy-start.8
  203.7 3.4 %copy-start.2 = (bf16[16,2,64,8,128]{4,3,2,0,1:T(8,128)(2,1)S(1)}, bf16[16,2,64,8,128]{4,3,2,0,1:T(8,128)(2,1)}, u32[]{:S(2)}) copy-start(bf16[16,2,64,8,128]{4,3,2,0,1:T(8,128)(2,1)} %copy.23) | copy-start | bytes 12582916
  212.9 2.0 copy-start
  212.9 3.6 %copy-start.1 = (bf16[2,1024,8,128]{3,2,1,0:T(8,128)(2,1)}, bf16[2,1024,8,128]{3,2,1,0:T(8,128)(2,1)S(1)}, u32[]{:S(2)}) copy-start(bf16[2,1024,8,128]{3,2,1,0:T(8,128)(2,1)S(1)} %get-tuple-element.10) | copy-start | bytes 12582916
where the time goes:
time: 239 us; the launch traced here: 238 us
  blocking collectives  103 us (43%)
  waiting for transfers between devices  60.7 us (25%)
  matrix products  49.2 us (21%)
  local copies, waits for them, and re-layouts  11 us (5%)
  other arithmetic  6.7 us (3%)
  starting transfers between devices  6.67 us (3%)
    all_to_all x1, blocking collectives, per_device(): keys_old = lax.all_to_all(k_cache, 'cp', 0, 1, tiled=True)  103 us
    all_to_all x1, waiting for transfers between devices, per_device(): vals_old = lax.all_to_all(v_cache, 'cp', 0, 1, tiled=True)  60.7 us
    dot_general x1, matrix products, decode_local(): jnp.dot(attended, w_o, preferred_element_type=jnp.float32)  20.2 us
    dot_general x1, matrix products, project(): jnp.dot(normed, w_q, preferred_element_type=jnp.float32)  19.5 us
    all_to_all x1, starting transfers between devices, per_device(): vals_old = lax.all_to_all(v_cache, 'cp', 0, 1, tiled=True)  6.67 us
    select_n x1, other arithmetic, decode_local(): jnp.where(slot_idx < pos_col, keys_old, jnp.where(slot_idx == pos_col, ke...  5.72 us
    dot_general x1, matrix products, project(): jnp.dot(normed, w_v, preferred_element_type=jnp.float32)  5.63 us
  transfers between devices with their start and end apart: 1, of which 1 were waited for; matrix products, arithmetic and copies ran while one was open for 13% of the time, Pallas kernels for 0%

commit v1 on v0

v1 whole, which is shorter than its diff:
```python
import functools
import math
import jax
import jax.numpy as jnp
from jax import lax
from jax.experimental import pallas as pl
from jax.experimental.pallas import tpu as pltpu
from jax.sharding import PartitionSpec as P

RMS_EPS = 1e-6
ROPE_THETA = 1000000.0
MASKED = -1e30
RING = 8
PACK = 5
TILE = 512
LHS_ROWS = 16
MESH = pl.DeviceIdType.MESH


def decode_kernel(dims, lens_ref, x_ref, gain_ref, bq_ref, bk_ref, bv_ref, k_ref, v_ref, wq_ref, wk_ref, wv_ref, wo_ref,
                  y_ref, k_land, v_land,
                  ring, scores, h_ref, acc, acc_kv, q_raw, q_rot, k_raw, v_raw, o_acc, m_acc, l_acc, o_row,
                  ring_sem, own_sem, send_sem, recv_sem):
    n, rows, span, kv_heads, head_dim, heads = dims
    group = heads // kv_heads
    width = heads * head_dim
    kv_width = kv_heads * head_dim
    chunk = span * kv_heads
    depth = x_ref.shape[1]
    half_dim = head_dim // 2
    block = depth // 10
    group_id = lax.axis_index("dp")
    me = lax.axis_index("cp")

    barrier = pltpu.get_barrier_semaphore()

    def greet(d, carry):
        peer = lax.rem(me + d, n)
        pl.semaphore_signal(barrier, inc=1, device_id=(group_id, peer), device_id_type=MESH)
        return carry

    lax.fori_loop(1, n, greet, 0)

    def weight_copies(b):
        slot = ring.at[b % RING]
        if b < 4:
            src = wk_ref if b < 2 else wv_ref
            base = (b % 2) * PACK
            return [pltpu.make_async_copy(src.at[pl.ds((base + c) * block, block)],
                                          slot.at[:, pl.ds(c * kv_width, kv_width)], ring_sem.at[b % RING, c])
                    for c in range(PACK)]
        src, r = (wq_ref, b - 4) if b < 14 else (wo_ref, b - 14)
        return [pltpu.make_async_copy(src.at[pl.ds(r * block, block)], slot, ring_sem.at[b % RING, 0])]

    def start_weights(b):
        for copy in weight_copies(b):
            copy.start()

    def wait_weights(b):
        for copy in weight_copies(b):
            copy.wait()

    def own_copy(c, src, land):
        return pltpu.make_async_copy(src.at[pl.ds(me * rows, rows)], land.at[:, pl.ds(me * chunk, chunk)], own_sem.at[c])

    def push(c, src, land, d):
        peer = lax.rem(me + d, n)
        return pltpu.make_async_remote_copy(
            src_ref=src.at[pl.ds(peer * rows, rows)],
            dst_ref=land.at[:, pl.ds(me * chunk, chunk)],
            send_sem=send_sem.at[c, d], recv_sem=recv_sem.at[c, me],
            device_id=(group_id, peer), device_id_type=MESH)

    def arrival(c, land, source):
        return pltpu.make_async_remote_copy(
            src_ref=land.at[:, pl.ds(source * chunk, chunk)],
            dst_ref=land.at[:, pl.ds(source * chunk, chunk)],
            send_sem=send_sem.at[c, 0], recv_sem=recv_sem.at[c, source],
            device_id=(group_id, me), device_id_type=MESH)

    pl.semaphore_wait(barrier, n - 1)
    order = []
    for d in range(n // 2, 0, -1):
        order.append(d)
        if n - d != d:
            order.append(n - d)
    for c, (src, land) in enumerate(((k_ref, k_land), (v_ref, v_land))):
        for d in order:
            push(c, src, land, d).start()
    own_copy(0, k_ref, k_land).start()
    own_copy(1, v_ref, v_land).start()
    for b in range(RING):
        start_weights(b)

    x_wide = x_ref[...].astype(jnp.float32)
    mean_sq = jnp.mean(x_wide * x_wide, axis=-1, keepdims=True)
    normed = x_wide * lax.rsqrt(mean_sq + RMS_EPS) * gain_ref[...].astype(jnp.float32)
    h_ref[...] = jnp.concatenate([normed, jnp.zeros((LHS_ROWS - rows, depth), jnp.float32)], axis=0).astype(jnp.bfloat16)
    acc[...] = jnp.zeros_like(acc)
    acc_kv[...] = jnp.zeros_like(acc_kv)

    def multiply(lhs, slot, out, tile_count):
        def tile(t, carry):
            cols = pl.ds(pl.multiple_of(t * TILE, TILE), TILE)
            out[:, cols] += jnp.dot(lhs, ring[slot, :, cols], preferred_element_type=jnp.float32)
            return carry
        lax.fori_loop(0, tile_count, tile, 0)

    def multiply_kv(b):
        base = (b % 2) * PACK
        out = (b // 2) * kv_width
        slot = b % RING
        def part(c, carry):
            lhs = h_ref[:, pl.ds(pl.multiple_of((base + c) * block, block), block)]
            for t in range(kv_width // TILE):
                cols = pl.ds(out + t * TILE, TILE)
                src = pl.ds(pl.multiple_of(c * kv_width + t * TILE, TILE), TILE)
                acc_kv[:, cols] += jnp.dot(lhs, ring[slot, :, src], preferred_element_type=jnp.float32)
            return carry
        lax.fori_loop(0, PACK, part, 0)

    for b in range(4):
        wait_weights(b)
        multiply_kv(b)
        start_weights(b + RING)
    for b in range(4, 14):
        wait_weights(b)
        multiply(h_ref[:, pl.ds((b - 4) * block, block)], b % RING, acc, width // TILE)
        if b + RING < 22:
            start_weights(b + RING)

    lane = lax.broadcasted_iota(jnp.int32, (1, head_dim), 1)
    freq_idx = jnp.where(lane < half_dim, lane, lane - half_dim).astype(jnp.float32)
    inv_freq = jnp.exp(freq_idx * (-2.0 * math.log(ROPE_THETA) / head_dim))
    sign = jnp.where(lane < half_dim, -1.0, 1.0)
    for s in range(rows):
        for j in range(heads):
            cols = slice(j * head_dim, (j + 1) * head_dim)
            q_raw[s, pl.ds(j, 1), :] = acc[pl.ds(s, 1), cols] + bq_ref[:, cols].astype(jnp.float32)
        for j in range(kv_heads):
            cols = slice(j * head_dim, (j + 1) * head_dim)
            v_cols = slice(kv_width + j * head_dim, kv_width + (j + 1) * head_dim)
            k_raw[s, pl.ds(j, 1), :] = acc_kv[pl.ds(s, 1), cols] + bk_ref[:, cols].astype(jnp.float32)
            v_raw[s, pl.ds(j, 1), :] = acc_kv[pl.ds(s, 1), v_cols] + bv_ref[:, cols].astype(jnp.float32)
    for s in range(rows):
        angle = lens_ref[me * rows + s].astype(jnp.float32) * inv_freq
        cos_t = jnp.cos(angle)
        sin_t = jnp.sin(angle) * sign
        q_one = q_raw[s]
        q_rot[s] = (q_one * cos_t + pltpu.roll(q_one, half_dim, 1) * sin_t).astype(jnp.bfloat16)
        k_one = k_raw[s]
        k_raw[s] = (k_one * cos_t + pltpu.roll(k_one, half_dim, 1) * sin_t).astype(jnp.bfloat16).astype(jnp.float32)
        v_raw[s] = v_raw[s].astype(jnp.bfloat16).astype(jnp.float32)

    row_idx = lax.broadcasted_iota(jnp.int32, (span, kv_heads, head_dim), 0)
    col = lax.broadcasted_iota(jnp.int32, (heads, chunk), 1)
    head = lax.broadcasted_iota(jnp.int32, (heads, chunk), 0)
    own_head = (col % kv_heads) == (head // group)
    col_slot = col // kv_heads
    scale = head_dim ** -0.5

    def settle(land, s, source, fresh):
        place = pl.ds(pl.multiple_of(source * chunk, chunk), chunk)
        limit = lens_ref[me * rows + s] - source * span
        old = land[s, place, :].astype(jnp.float32).reshape(span, kv_heads, head_dim)
        kept = jnp.where(row_idx < limit, old, jnp.where(row_idx == limit, fresh[s][None], 0.0))
        kept = kept.reshape(chunk, head_dim).astype(jnp.bfloat16)
        land[s, place, :] = kept
        return kept, place, limit

    def lane_fold(op, values):
        out = values[:, :head_dim]
        for t in range(1, chunk // head_dim):
            out = op(out, values[:, t * head_dim:(t + 1) * head_dim])
        return out

    def score_chunk(source):
        for s in range(rows):
            keys, place, limit = settle(k_land, s, source, k_raw)
            sc = lax.dot_general(q_rot[s], keys, (((1,), (1,)), ((), ())), preferred_element_type=jnp.float32) * scale
            sc = jnp.where(own_head & (col_slot <= limit), sc, MASKED)
            scores[s, :, place] = sc
            m_acc[s] = jnp.maximum(m_acc[s], lane_fold(jnp.maximum, sc))

    def value_chunk(source):
        for s in range(rows):
            vals, place, limit = settle(v_land, s, source, v_raw)
            e = jnp.exp(scores[s, :, place] - m_acc[s][:, :1])
            l_acc[s] += lane_fold(jnp.add, e)
            o_acc[s] += jnp.dot(e.astype(jnp.bfloat16), vals, preferred_element_type=jnp.float32)

    m_acc[...] = jnp.full_like(m_acc, MASKED)
    l_acc[...] = jnp.zeros_like(l_acc)
    o_acc[...] = jnp.zeros_like(o_acc)

    own_copy(0, k_ref, k_land).wait()
    score_chunk(me)
    for d in order:
        source = lax.rem(me - d + n, n)
        arrival(0, k_land, source).wait_recv()
        score_chunk(source)
    for s in range(rows):
        m_acc[s] = jnp.broadcast_to(jnp.max(m_acc[s], axis=-1, keepdims=True), (heads, head_dim))
    own_copy(1, v_ref, v_land).wait()
    value_chunk(me)
    for d in order:
        source = lax.rem(me - d + n, n)
        arrival(1, v_land, source).wait_recv()
        value_chunk(source)

    o_row[...] = jnp.zeros_like(o_row)
    for s in range(rows):
        l_all = jnp.sum(l_acc[s], axis=-1, keepdims=True)
        q_raw[s] = o_acc[s] / l_all
        for j in range(heads):
            o_row[pl.ds(s, 1), j * head_dim:(j + 1) * head_dim] = q_raw[s, pl.ds(j, 1), :]
    h_ref[...] = o_row[...].astype(jnp.bfloat16)
    acc[...] = jnp.zeros_like(acc)
    for b in range(14, 24):
        wait_weights(b)
        multiply(h_ref[:, pl.ds((b - 14) * block, block)], b % RING, acc, width // TILE)
        if b + RING < 24:
            start_weights(b + RING)
    y_ref[...] = (x_ref[...].astype(jnp.float32) + acc[:rows, :]).astype(jnp.bfloat16)
    for c, (src, land) in enumerate(((k_ref, k_land), (v_ref, v_land))):
        for d in order:
            push(c, src, land, d).wait_send()


def solution(mesh):
    batch_spec = P(('dp', 'cp'))
    seq_spec = P('dp', 'cp')
    whole = P()
    n = mesh.shape['cp']

    def per_device(x_tok, prompt_lens, k_cache, v_cache, norm_gain, w_q, b_q, w_k, b_k, w_v, b_v, w_o):
        rows, depth = x_tok.shape
        batch, span, kv_heads, head_dim = k_cache.shape
        width = w_q.shape[1]
        heads = width // head_dim
        chunk = span * kv_heads
        kv_width = kv_heads * head_dim
        block = depth // 10
        dims = (n, rows, span, kv_heads, head_dim, heads)
        vmem = pl.BlockSpec(memory_space=pltpu.VMEM)
        smem = pl.BlockSpec(memory_space=pltpu.SMEM)
        hbm = pl.BlockSpec(memory_space=pl.ANY)
        bf16, f32 = jnp.bfloat16, jnp.float32
        y, k_all, v_all = pl.pallas_call(
            functools.partial(decode_kernel, dims),
            out_shape=(jax.ShapeDtypeStruct((rows, depth), bf16),
                       pltpu.VMEM((rows, n * chunk, head_dim), bf16),
                       pltpu.VMEM((rows, n * chunk, head_dim), bf16)),
            in_specs=[smem] + [vmem] * 5 + [hbm] * 6,
            out_specs=(vmem, vmem, vmem),
            scratch_shapes=[
                pltpu.VMEM((RING, block, width), bf16),
                pltpu.VMEM((rows, heads, n * chunk), f32),
                pltpu.VMEM((LHS_ROWS, depth), bf16),
                pltpu.VMEM((LHS_ROWS, width), f32),
                pltpu.VMEM((LHS_ROWS, 2 * kv_width), f32),
                pltpu.VMEM((rows, heads, head_dim), f32),
                pltpu.VMEM((rows, heads, head_dim), bf16),
                pltpu.VMEM((rows, kv_heads, head_dim), f32),
                pltpu.VMEM((rows, kv_heads, head_dim), f32),
                pltpu.VMEM((rows, heads, head_dim), f32),
                pltpu.VMEM((rows, heads, head_dim), f32),
                pltpu.VMEM((rows, heads, head_dim), f32),
                pltpu.VMEM((LHS_ROWS, width), f32),
                pltpu.SemaphoreType.DMA((RING, PACK)),
                pltpu.SemaphoreType.DMA((2,)),
                pltpu.SemaphoreType.DMA((2, n)),
                pltpu.SemaphoreType.DMA((2, n)),
            ],
            compiler_params=pltpu.CompilerParams(collective_id=0, has_side_effects=True, vmem_limit_bytes=50 * 1024 * 1024),
            cost_estimate=pl.CostEstimate(flops=1 << 30, bytes_accessed=1 << 27, transcendentals=0),
        )(prompt_lens, x_tok, norm_gain[None], b_q[None], b_k[None], b_v[None],
          k_cache.reshape(batch, chunk, head_dim), v_cache.reshape(batch, chunk, head_dim), w_q, w_k, w_v, w_o)
        shape = (rows, n * span, kv_heads, head_dim)
        return y, k_all.reshape(shape), v_all.reshape(shape)

    return jax.shard_map(per_device, mesh=mesh, in_specs=(batch_spec, P('dp'), seq_spec, seq_spec, whole, whole, whole, whole, whole, whole, whole, whole), out_specs=(batch_spec, batch_spec, batch_spec), check_vma=False)
```

time: 239 us -> 228 us (0.954); the launches traced: 238 us -> 223 us
  Pallas kernels: 0 us -> 213 us
  blocking collectives: 103 us -> 0 us
  waiting for transfers between devices: 60.7 us -> 0 us
  matrix products: 49.2 us -> 0 us
  other arithmetic: 6.7 us -> 0 us
  starting transfers between devices: 6.67 us -> 0 us
    pallas_call x0 -> x1, Pallas kernels: none -> 213 us  [per_device(): pl.pallas_call(functools.partial(decode_kernel, dims), out_shape=(jax.Sha...]
    all_to_all x1 -> x0, blocking collectives: 103 us -> none  [per_device(): keys_old = lax.all_to_all(k_cache, 'cp', 0, 1, tiled=True)]
    all_to_all x1 -> x0, waiting for transfers between devices: 60.7 us -> none  [per_device(): vals_old = lax.all_to_all(v_cache, 'cp', 0, 1, tiled=True)]
    dot_general x6 -> x0, matrix products: 49.2 us -> none  [the longest x1 20.2 us: decode_local(): jnp.dot(attended, w_o, preferred_element_type=jnp.float32)]
    all_to_all x2 -> x0, local copies, waits for them, and re-layouts: 7.27 us -> none  [the longest x1 4.65 us: per_device(): keys_old = lax.all_to_all(k_cache, 'cp', 0, 1, tiled=True)]
    all_to_all x1 -> x0, starting transfers between devices: 6.67 us -> none  [per_device(): vals_old = lax.all_to_all(v_cache, 'cp', 0, 1, tiled=True)]
    select_n x1 -> x0, other arithmetic: 5.72 us -> none  [decode_local(): jnp.where(slot_idx < pos_col, keys_old, jnp.where(slot_idx == pos_col, ke...]
    broadcast_in_dim x0 -> x4, local copies, waits for them, and re-layouts: none -> 5.19 us  [the longest x1 1.32 us: per_device(): norm_gain[None]]
  transfers between devices with their start and end apart: 1 -> 0, of which waited for: 1 -> 0; matrix products, arithmetic and copies ran while one was open for 13% -> 0% of each run, Pallas kernels for 0% -> 0%
where the time goes in v1:
time: 228 us; the launch traced here: 223 us
  Pallas kernels  213 us (93%)
  local copies, waits for them, and re-layouts  9.83 us (4%)
    pallas_call x1, Pallas kernels, per_device(): pl.pallas_call(functools.partial(decode_kernel, dims), out_shape=(jax.Sha...  213 us
    unnamed x5, local copies, waits for them, and re-layouts  4.64 us

profile of v1, /device:TPU:53, one launch (start us, length us, event | category | flops | bytes accessed | tf_op | source)
XLA Modules:
  0.0 223.1 jit_solution(6939379288463482408)
XLA Ops:
  0.6 1.3 broadcast_in_dim.14.bk_ref
  1.9 1.3 broadcast_in_dim.15.bv_ref
  3.2 1.3 broadcast_in_dim.12.gain_ref
  4.5 1.3 broadcast_in_dim.13.bq_ref
  5.8 212.6 %shard_map.139 = (bf16[2,5120]{1,0:T(2,128)(2,1)}, bf16[2,8192,128]{2,1,0:T(8,128)(2,1)S(1)}, bf16[2,8192,128]{2,1,0:T(8,128)(2,1)S(1)}) custom-call(s32[32]{0:T(128)} %lens_ref.1, bf16[2,5120]{1,0:T(2,128)(2,1)} %x_ref.1, bf16[1,5120]{1,0:T(2,128)(2,1)} %broadcast_in_dim.12.gain_ref, bf16[1,5120]{1,0:T(2,128)(2,1)} %broadcast_in_dim.13.bq_ref, ...), custom_call_target="tpu_custom_call" | custom-call | flops 1073741824 | bytes 134217728 | tf_op jit(solution)/shard_map/pallas_call | solution.py:249
  218.5 2.0 copy.18
  220.5 0.0 copy-start
  220.5 2.0 copy.19
  222.5 0.0 copy-done
  222.5 0.6 copy.20
Async XLA Ops:
  220.5 2.0 copy-start

commit v2 on v1

--- a/solution.py
+++ b/solution.py
@@ -10,17 +10,18 @@
 RMS_EPS = 1e-6
 ROPE_THETA = 1000000.0
 MASKED = -1e30
-RING = 8
+RING = 9
 PACK = 5
 TILE = 512
 LHS_ROWS = 16
 MESH = pl.DeviceIdType.MESH
 
 
-def decode_kernel(dims, lens_ref, x_ref, gain_ref, bq_ref, bk_ref, bv_ref, k_ref, v_ref, wq_ref, wk_ref, wv_ref, wo_ref,
-                  y_ref, k_land, v_land,
-                  ring, scores, h_ref, acc, acc_kv, q_raw, q_rot, k_raw, v_raw, o_acc, m_acc, l_acc, o_row,
-                  ring_sem, own_sem, send_sem, recv_sem):
+def exchange_kernel(dims, lens_hbm, x_hbm, gain_hbm, bq_hbm, bk_hbm, bv_hbm, k_ref, v_ref, wq_ref, wk_ref, wv_ref, wo_ref,
+                    o_ref, k_land, v_land, ring,
+                    lens_ref, x_ref, gain_ref, bq_ref, bk_ref, bv_ref,
+                    scores, h_ref, acc, acc_kv, q_raw, q_rot, k_raw, v_raw, o_acc, m_acc, l_acc, o_row,
+                    small_sem, ring_sem, own_sem, send_sem, recv_sem):
     n, rows, span, kv_heads, head_dim, heads = dims
     group = heads // kv_heads
     width = heads * head_dim
@@ -89,12 +90,18 @@
             push(c, src, land, d).start()
     own_copy(0, k_ref, k_land).start()
     own_copy(1, v_ref, v_land).start()
+    small = [pltpu.make_async_copy(src, dst, small_sem.at[i]) for i, (src, dst) in enumerate((
+        (lens_hbm, lens_ref), (x_hbm, x_ref), (gain_hbm, gain_ref), (bq_hbm, bq_ref), (bk_hbm, bk_ref), (bv_hbm, bv_ref)))]
+    for copy in small:
+        copy.start()
     for b in range(RING):
         start_weights(b)
+    for copy in small:
+        copy.wait()
 
     x_wide = x_ref[...].astype(jnp.float32)
     mean_sq = jnp.mean(x_wide * x_wide, axis=-1, keepdims=True)
-    normed = x_wide * lax.rsqrt(mean_sq + RMS_EPS) * gain_ref[...].astype(jnp.float32)
+    normed = x_wide * lax.rsqrt(mean_sq + RMS_EPS) * gain_ref[...].astype(jnp.float32).reshape(1, depth)
     h_ref[...] = jnp.concatenate([normed, jnp.zeros((LHS_ROWS - rows, depth), jnp.float32)], axis=0).astype(jnp.bfloat16)
     acc[...] = jnp.zeros_like(acc)
     acc_kv[...] = jnp.zeros_like(acc_kv)
@@ -126,31 +133,31 @@
     for b in range(4, 14):
         wait_weights(b)
         multiply(h_ref[:, pl.ds((b - 4) * block, block)], b % RING, acc, width // TILE)
-        if b + RING < 22:
+        if b + RING < 14 + RING:
             start_weights(b + RING)
 
     lane = lax.broadcasted_iota(jnp.int32, (1, head_dim), 1)
     freq_idx = jnp.where(lane < half_dim, lane, lane - half_dim).astype(jnp.float32)
     inv_freq = jnp.exp(freq_idx * (-2.0 * math.log(ROPE_THETA) / head_dim))
     sign = jnp.where(lane < half_dim, -1.0, 1.0)
+    q_bias = bq_ref[...].astype(jnp.float32).reshape(heads, head_dim)
+    k_bias = bk_ref[...].astype(jnp.float32).reshape(kv_heads, head_dim)
+    v_bias = bv_ref[...].astype(jnp.float32).reshape(kv_heads, head_dim)
     for s in range(rows):
         for j in range(heads):
-            cols = slice(j * head_dim, (j + 1) * head_dim)
-            q_raw[s, pl.ds(j, 1), :] = acc[pl.ds(s, 1), cols] + bq_ref[:, cols].astype(jnp.float32)
+            q_raw[s, pl.ds(j, 1), :] = acc[pl.ds(s, 1), j * head_dim:(j + 1) * head_dim]
         for j in range(kv_heads):
-            cols = slice(j * head_dim, (j + 1) * head_dim)
-            v_cols = slice(kv_width + j * head_dim, kv_width + (j + 1) * head_dim)
-            k_raw[s, pl.ds(j, 1), :] = acc_kv[pl.ds(s, 1), cols] + bk_ref[:, cols].astype(jnp.float32)
-            v_raw[s, pl.ds(j, 1), :] = acc_kv[pl.ds(s, 1), v_cols] + bv_ref[:, cols].astype(jnp.float32)
+            k_raw[s, pl.ds(j, 1), :] = acc_kv[pl.ds(s, 1), j * head_dim:(j + 1) * head_dim]
+            v_raw[s, pl.ds(j, 1), :] = acc_kv[pl.ds(s, 1), kv_width + j * head_dim:kv_width + (j + 1) * head_dim]
     for s in range(rows):
         angle = lens_ref[me * rows + s].astype(jnp.float32) * inv_freq
         cos_t = jnp.cos(angle)
         sin_t = jnp.sin(angle) * sign
-        q_one = q_raw[s]
+        q_one = q_raw[s] + q_bias
         q_rot[s] = (q_one * cos_t + pltpu.roll(q_one, half_dim, 1) * sin_t).astype(jnp.bfloat16)
-        k_one = k_raw[s]
+        k_one = k_raw[s] + k_bias
         k_raw[s] = (k_one * cos_t + pltpu.roll(k_one, half_dim, 1) * sin_t).astype(jnp.bfloat16).astype(jnp.float32)
-        v_raw[s] = v_raw[s].astype(jnp.bfloat16).astype(jnp.float32)
+        v_raw[s] = (v_raw[s] + v_bias).astype(jnp.bfloat16).astype(jnp.float32)
 
     row_idx = lax.broadcasted_iota(jnp.int32, (span, kv_heads, head_dim), 0)
     col = lax.broadcasted_iota(jnp.int32, (heads, chunk), 1)
@@ -214,17 +221,44 @@
         q_raw[s] = o_acc[s] / l_all
         for j in range(heads):
             o_row[pl.ds(s, 1), j * head_dim:(j + 1) * head_dim] = q_raw[s, pl.ds(j, 1), :]
-    h_ref[...] = o_row[...].astype(jnp.bfloat16)
-    acc[...] = jnp.zeros_like(acc)
-    for b in range(14, 24):
+    o_ref[...] = o_row[...].astype(jnp.bfloat16)
+    for b in range(14, 14 + RING):
         wait_weights(b)
-        multiply(h_ref[:, pl.ds((b - 14) * block, block)], b % RING, acc, width // TILE)
-        if b + RING < 24:
-            start_weights(b + RING)
-    y_ref[...] = (x_ref[...].astype(jnp.float32) + acc[:rows, :]).astype(jnp.bfloat16)
     for c, (src, land) in enumerate(((k_ref, k_land), (v_ref, v_land))):
         for d in order:
             push(c, src, land, d).wait_send()
+
+
+def output_kernel(first, o_ref, k_land, v_land, ring, x_hbm, wo_ref, y_ref, k_out, v_out, x_ref, extra, acc, sem):
+    rows, depth = x_ref.shape
+    block, width = extra.shape[1:]
+    resident = ring.shape[0]
+    tail = [pltpu.make_async_copy(wo_ref.at[pl.ds((resident + i) * block, block)], extra.at[i], sem.at[i])
+            for i in range(extra.shape[0])]
+    rest = [pltpu.make_async_copy(x_hbm, x_ref, sem.at[len(tail)]),
+            pltpu.make_async_copy(k_land, k_out, sem.at[len(tail) + 1]),
+            pltpu.make_async_copy(v_land, v_out, sem.at[len(tail) + 2])]
+    for copy in tail + rest:
+        copy.start()
+    acc[...] = jnp.zeros_like(acc)
+
+    def multiply(r, weights):
+        lhs = o_ref[:, r * block:(r + 1) * block]
+
+        def tile(t, carry):
+            cols = pl.ds(pl.multiple_of(t * TILE, TILE), TILE)
+            acc[:, cols] += jnp.dot(lhs, weights[:, cols], preferred_element_type=jnp.float32)
+            return carry
+        lax.fori_loop(0, width // TILE, tile, 0)
+
+    for r in range(resident):
+        multiply(r, ring.at[(first + r) % resident])
+    for i, copy in enumerate(tail):
+        copy.wait()
+        multiply(resident + i, extra.at[i])
+    for copy in rest:
+        copy.wait()
+    y_ref[...] = (x_ref[...].astype(jnp.float32) + acc[:rows, :]).astype(jnp.bfloat16)
 
 
 def solution(mesh):
@@ -246,15 +280,20 @@
         smem = pl.BlockSpec(memory_space=pltpu.SMEM)
         hbm = pl.BlockSpec(memory_space=pl.ANY)
         bf16, f32 = jnp.bfloat16, jnp.float32
-        y, k_all, v_all = pl.pallas_call(
-            functools.partial(decode_kernel, dims),
-            out_shape=(jax.ShapeDtypeStruct((rows, depth), bf16),
-                       pltpu.VMEM((rows, n * chunk, head_dim), bf16),
-                       pltpu.VMEM((rows, n * chunk, head_dim), bf16)),
-            in_specs=[smem] + [vmem] * 5 + [hbm] * 6,
-            out_specs=(vmem, vmem, vmem),
+        land = (rows, n * chunk, head_dim)
+        o_rows, k_all, v_all, ring = pl.pallas_call(
+            functools.partial(exchange_kernel, dims),
+            out_shape=(pltpu.VMEM((LHS_ROWS, width), bf16), pltpu.VMEM(land, bf16), pltpu.VMEM(land, bf16),
+                       pltpu.VMEM((RING, block, width), bf16)),
+            in_specs=[hbm] * 12,
+            out_specs=(vmem,) * 4,
             scratch_shapes=[
-                pltpu.VMEM((RING, block, width), bf16),
+                pltpu.SMEM((batch,), jnp.int32),
+                pltpu.VMEM((rows, depth), bf16),
+                pltpu.VMEM((depth,), bf16),
+                pltpu.VMEM((width,), bf16),
+                pltpu.VMEM((kv_width,), bf16),
+                pltpu.VMEM((kv_width,), bf16),
                 pltpu.VMEM((rows, heads, n * chunk), f32),
                 pltpu.VMEM((LHS_ROWS, depth), bf16),
                 pltpu.VMEM((LHS_ROWS, width), f32),
@@ -267,16 +306,32 @@
                 pltpu.VMEM((rows, heads, head_dim), f32),
                 pltpu.VMEM((rows, heads, head_dim), f32),
                 pltpu.VMEM((LHS_ROWS, width), f32),
+                pltpu.SemaphoreType.DMA((6,)),
                 pltpu.SemaphoreType.DMA((RING, PACK)),
                 pltpu.SemaphoreType.DMA((2,)),
                 pltpu.SemaphoreType.DMA((2, n)),
                 pltpu.SemaphoreType.DMA((2, n)),
             ],
-            compiler_params=pltpu.CompilerParams(collective_id=0, has_side_effects=True, vmem_limit_bytes=50 * 1024 * 1024),
+            compiler_params=pltpu.CompilerParams(collective_id=0, has_side_effects=True, vmem_limit_bytes=8 * 1024 * 1024),
             cost_estimate=pl.CostEstimate(flops=1 << 30, bytes_accessed=1 << 27, transcendentals=0),
-        )(prompt_lens, x_tok, norm_gain[None], b_q[None], b_k[None], b_v[None],
+        )(prompt_lens, x_tok, norm_gain, b_q, b_k, b_v,
           k_cache.reshape(batch, chunk, head_dim), v_cache.reshape(batch, chunk, head_dim), w_q, w_k, w_v, w_o)
+        extra = depth // block - RING
+        y, k_out, v_out = pl.pallas_call(
+            functools.partial(output_kernel, 14),
+            out_shape=(jax.ShapeDtypeStruct((rows, depth), bf16), jax.ShapeDtypeStruct(land, bf16), jax.ShapeDtypeStruct(land, bf16)),
+            in_specs=[vmem] * 4 + [hbm] * 2,
+            out_specs=(vmem, hbm, hbm),
+            scratch_shapes=[
+                pltpu.VMEM((rows, depth), bf16),
+                pltpu.VMEM((extra, block, width), bf16),
+                pltpu.VMEM((LHS_ROWS, depth), f32),
+                pltpu.SemaphoreType.DMA((extra + 3,)),
+            ],
+            compiler_params=pltpu.CompilerParams(vmem_limit_bytes=(extra * 6 + 2) * 1024 * 1024),
+            cost_estimate=pl.CostEstimate(flops=1 << 30, bytes_accessed=1 << 25, transcendentals=0),
+        )(*[pltpu.with_memory_space_constraint(a, pltpu.VMEM) for a in (o_rows, k_all, v_all, ring)], x_tok, w_o)
         shape = (rows, n * span, kv_heads, head_dim)
-        return y, k_all.reshape(shape), v_all.reshape(shape)
+        return y, k_out.reshape(shape), v_out.reshape(shape)
 
     return jax.shard_map(per_device, mesh=mesh, in_specs=(batch_spec, P('dp'), seq_spec, seq_spec, whole, whole, whole, whole, whole, whole, whole, whole), out_specs=(batch_spec, batch_spec, batch_spec), check_vma=False)

time: 228 us -> 217 us (0.952)
  local copies, waits for them, and re-layouts: 9.83 us -> 0 us
    broadcast_in_dim x4 -> x0, local copies, waits for them, and re-layouts: 5.19 us -> none  [the longest x1 1.32 us: per_device(): norm_gain[None]]
    unnamed x5 -> x0, local copies, waits for them, and re-layouts: 4.64 us -> none
    pallas_call x1 -> x2, Pallas kernels: 213 us -> 212 us  [the longest x1 193 us: per_device(): pl.pallas_call(functools.partial(exchange_kernel, dims), out_shape=(pltpu...]
where the time goes in v2:
time: 217 us; the launch traced here: 213 us
  Pallas kernels  212 us (98%)
    pallas_call x1, Pallas kernels, per_device(): pl.pallas_call(functools.partial(exchange_kernel, dims), out_shape=(pltpu...  193 us
    pallas_call x1, Pallas kernels, per_device(): pl.pallas_call(functools.partial(output_kernel, 14), out_shape=(jax.Shape...  19.5 us

profile of v2, /device:TPU:53, one launch (start us, length us, event | category | flops | bytes accessed | tf_op | source)
XLA Modules:
  0.0 212.7 jit_solution(11687739610066738675)
XLA Ops:
  0.6 192.6 %shard_map.139 = (bf16[16,5120]{1,0:T(8,128)(2,1)S(1)}, bf16[2,8192,128]{2,1,0:T(8,128)(2,1)S(1)}, bf16[2,8192,128]{2,1,0:T(8,128)(2,1)S(1)}, bf16[9,512,5120]{2,1,0:T(8,128)(2,1)S(1)}) custom-call(s32[32]{0:T(128)} %lens_hbm.1, bf16[2,5120]{1,0:T(2,128)(2,1)} %x_hbm.3, bf16[5120]{0:T(1024)(128)(2,1)} %gain_hbm.1, bf16[5120]{0:T(1024)(128)(2,1)} %bq_hbm.1, ...), custom_call_target="tpu_custom_call" | custom-call | flops 1073741824 | bytes 134217728 | tf_op jit(solution)/shard_map/pallas_call | solution.py:284
  193.2 19.5 %shard_map.140 = (bf16[2,5120]{1,0:T(2,128)(2,1)}, bf16[2,8192,128]{2,1,0:T(8,128)(2,1)}, bf16[2,8192,128]{2,1,0:T(8,128)(2,1)}) custom-call(bf16[16,5120]{1,0:T(8,128)(2,1)S(1)} %get-tuple-element.10.o_ref, bf16[2,8192,128]{2,1,0:T(8,128)(2,1)S(1)} %get-tuple-element.11.k_land, bf16[2,8192,128]{2,1,0:T(8,128)(2,1)S(1)} %get-tuple-element.12.v_land, ...), custom_call_target="tpu_custom_call" | custom-call | flops 1073741824 | bytes 33554432 | tf_op jit(solution)/shard_map/pallas_call | solution.py:320

commit v3 on v2

--- a/solution.py
+++ b/solution.py
@@ -13,6 +13,7 @@
 RING = 9
 PACK = 5
 TILE = 512
+OUT_TILE = 512
 LHS_ROWS = 16
 MESH = pl.DeviceIdType.MESH
 
@@ -245,11 +246,9 @@
     def multiply(r, weights):
         lhs = o_ref[:, r * block:(r + 1) * block]
 
-        def tile(t, carry):
-            cols = pl.ds(pl.multiple_of(t * TILE, TILE), TILE)
+        for t in range(width // OUT_TILE):
+            cols = slice(t * OUT_TILE, (t + 1) * OUT_TILE)
             acc[:, cols] += jnp.dot(lhs, weights[:, cols], preferred_element_type=jnp.float32)
-            return carry
-        lax.fori_loop(0, width // TILE, tile, 0)
 
     for r in range(resident):
         multiply(r, ring.at[(first + r) % resident])

time: 217 us -> 205 us (0.945)
  the two profiles are of different devices: /device:TPU:53 before, /device:TPU:124 now
where the time goes in v3:
time: 205 us
  Pallas kernels  204 us (100%)
    pallas_call x1, Pallas kernels, per_device(): pl.pallas_call(functools.partial(exchange_kernel, dims), out_shape=(pltpu...  197 us
    pallas_call x1, Pallas kernels, per_device(): pl.pallas_call(functools.partial(output_kernel, 14), out_shape=(jax.Shape...  7.55 us

profile of v3, /device:TPU:124, one launch (start us, length us, event | category | flops | bytes accessed | tf_op | source)
XLA Modules:
  0.0 204.9 jit_solution(10499419721949138924)
XLA Ops:
  0.6 196.7 %shard_map.139 = (bf16[16,5120]{1,0:T(8,128)(2,1)S(1)}, bf16[2,8192,128]{2,1,0:T(8,128)(2,1)S(1)}, bf16[2,8192,128]{2,1,0:T(8,128)(2,1)S(1)}, bf16[9,512,5120]{2,1,0:T(8,128)(2,1)S(1)}) custom-call(s32[32]{0:T(128)} %lens_hbm.1, bf16[2,5120]{1,0:T(2,128)(2,1)} %x_hbm.3, bf16[5120]{0:T(1024)(128)(2,1)} %gain_hbm.1, bf16[5120]{0:T(1024)(128)(2,1)} %bq_hbm.1, ...), custom_call_target="tpu_custom_call" | custom-call | flops 1073741824 | bytes 134217728 | tf_op jit(solution)/shard_map/pallas_call | solution.py:283
  197.3 7.5 %shard_map.140 = (bf16[2,5120]{1,0:T(2,128)(2,1)}, bf16[2,8192,128]{2,1,0:T(8,128)(2,1)}, bf16[2,8192,128]{2,1,0:T(8,128)(2,1)}) custom-call(bf16[16,5120]{1,0:T(8,128)(2,1)S(1)} %get-tuple-element.10.o_ref, bf16[2,8192,128]{2,1,0:T(8,128)(2,1)S(1)} %get-tuple-element.11.k_land, bf16[2,8192,128]{2,1,0:T(8,128)(2,1)S(1)} %get-tuple-element.12.v_land, ...), custom_call_target="tpu_custom_call" | custom-call | flops 1073741824 | bytes 33554432 | tf_op jit(solution)/shard_map/pallas_call | solution.py:319

commit v4 on v3

--- a/solution.py
+++ b/solution.py
@@ -15,6 +15,7 @@
 TILE = 512
 OUT_TILE = 512
 LHS_ROWS = 16
+CORES = 2
 MESH = pl.DeviceIdType.MESH
 
 
@@ -62,15 +63,20 @@
         for copy in weight_copies(b):
             copy.wait()
 
+    def partner(i):
+        offset, flip = pairs[i]
+        chip = lax.rem(lax.div(me, CORES) + offset + n // CORES, n // CORES)
+        return chip * CORES + lax.rem(lax.rem(me, CORES) + flip, CORES)
+
     def own_copy(c, src, land):
         return pltpu.make_async_copy(src.at[pl.ds(me * rows, rows)], land.at[:, pl.ds(me * chunk, chunk)], own_sem.at[c])
 
-    def push(c, src, land, d):
-        peer = lax.rem(me + d, n)
+    def push(c, src, land, i):
+        peer = partner(i)
         return pltpu.make_async_remote_copy(
             src_ref=src.at[pl.ds(peer * rows, rows)],
             dst_ref=land.at[:, pl.ds(me * chunk, chunk)],
-            send_sem=send_sem.at[c, d], recv_sem=recv_sem.at[c, me],
+            send_sem=send_sem.at[c, i], recv_sem=recv_sem.at[c, me],
             device_id=(group_id, peer), device_id_type=MESH)
 
     def arrival(c, land, source):
@@ -81,14 +87,17 @@
             device_id=(group_id, me), device_id_type=MESH)
 
     pl.semaphore_wait(barrier, n - 1)
-    order = []
-    for d in range(n // 2, 0, -1):
-        order.append(d)
-        if n - d != d:
-            order.append(n - d)
-    for c, (src, land) in enumerate(((k_ref, k_land), (v_ref, v_land))):
-        for d in order:
-            push(c, src, land, d).start()
+    chips = n // CORES
+    pairs = [(0, 1)]
+    for d in range(1, (chips - 1) // 2 + 1):
+        pairs += [(d, 0), (-d, 0), (d, 1), (-d, 1)]
+    near = len(pairs)
+    if chips % 2 == 0:
+        pairs += [(chips // 2, 0), (chips // 2, 1)]
+    for c, src, land, peers in ((0, k_ref, k_land, range(near)), (1, v_ref, v_land, range(near)),
+                                (0, k_ref, k_land, range(near, n - 1)), (1, v_ref, v_land, range(near, n - 1))):
+        for i in peers:
+            push(c, src, land, i).start()
     own_copy(0, k_ref, k_land).start()
     own_copy(1, v_ref, v_land).start()
     small = [pltpu.make_async_copy(src, dst, small_sem.at[i]) for i, (src, dst) in enumerate((
@@ -203,16 +212,16 @@
 
     own_copy(0, k_ref, k_land).wait()
     score_chunk(me)
-    for d in order:
-        source = lax.rem(me - d + n, n)
+    for i in range(n - 1):
+        source = partner(i)
         arrival(0, k_land, source).wait_recv()
         score_chunk(source)
     for s in range(rows):
         m_acc[s] = jnp.broadcast_to(jnp.max(m_acc[s], axis=-1, keepdims=True), (heads, head_dim))
     own_copy(1, v_ref, v_land).wait()
     value_chunk(me)
-    for d in order:
-        source = lax.rem(me - d + n, n)
+    for i in range(n - 1):
+        source = partner(i)
         arrival(1, v_land, source).wait_recv()
         value_chunk(source)
 
@@ -226,8 +235,8 @@
     for b in range(14, 14 + RING):
         wait_weights(b)
     for c, (src, land) in enumerate(((k_ref, k_land), (v_ref, v_land))):
-        for d in order:
-            push(c, src, land, d).wait_send()
+        for i in range(n - 1):
+            push(c, src, land, i).wait_send()
 
 
 def output_kernel(first, o_ref, k_land, v_land, ring, x_hbm, wo_ref, y_ref, k_out, v_out, x_ref, extra, acc, sem):

time: 205 us -> 201 us (0.980)
  the two profiles are of different devices: /device:TPU:124 before, /device:TPU:53 now
where the time goes in v4:
time: 201 us
  Pallas kernels  201 us (100%)
    pallas_call x1, Pallas kernels, per_device(): pl.pallas_call(functools.partial(exchange_kernel, dims), out_shape=(pltpu...  193 us
    pallas_call x1, Pallas kernels, per_device(): pl.pallas_call(functools.partial(output_kernel, 14), out_shape=(jax.Shape...  7.55 us

profile of v4, /device:TPU:53, one launch (start us, length us, event | category | flops | bytes accessed | tf_op | source)
XLA Modules:
  0.0 201.3 jit_solution(8164919384141036323)
XLA Ops:
  0.6 193.1 %shard_map.139 = (bf16[16,5120]{1,0:T(8,128)(2,1)S(1)}, bf16[2,8192,128]{2,1,0:T(8,128)(2,1)S(1)}, bf16[2,8192,128]{2,1,0:T(8,128)(2,1)S(1)}, bf16[9,512,5120]{2,1,0:T(8,128)(2,1)S(1)}) custom-call(s32[32]{0:T(128)} %lens_hbm.1, bf16[2,5120]{1,0:T(2,128)(2,1)} %x_hbm.3, bf16[5120]{0:T(1024)(128)(2,1)} %gain_hbm.1, bf16[5120]{0:T(1024)(128)(2,1)} %bq_hbm.1, ...), custom_call_target="tpu_custom_call" | custom-call | flops 1073741824 | bytes 134217728 | tf_op jit(solution)/shard_map/pallas_call | solution.py:292
  193.7 7.5 %shard_map.140 = (bf16[2,5120]{1,0:T(2,128)(2,1)}, bf16[2,8192,128]{2,1,0:T(8,128)(2,1)}, bf16[2,8192,128]{2,1,0:T(8,128)(2,1)}) custom-call(bf16[16,5120]{1,0:T(8,128)(2,1)S(1)} %get-tuple-element.10.o_ref, bf16[2,8192,128]{2,1,0:T(8,128)(2,1)S(1)} %get-tuple-element.11.k_land, bf16[2,8192,128]{2,1,0:T(8,128)(2,1)S(1)} %get-tuple-element.12.v_land, ...), custom_call_target="tpu_custom_call" | custom-call | flops 1073741824 | bytes 33554432 | tf_op jit(solution)/shard_map/pallas_call | solution.py:328

commit v5 on v4

--- a/solution.py
+++ b/solution.py
@@ -23,7 +23,7 @@
                     o_ref, k_land, v_land, ring,
                     lens_ref, x_ref, gain_ref, bq_ref, bk_ref, bv_ref,
                     scores, h_ref, acc, acc_kv, q_raw, q_rot, k_raw, v_raw, o_acc, m_acc, l_acc, o_row,
-                    small_sem, ring_sem, own_sem, send_sem, recv_sem):
+                    small_sem, ring_sem, own_sem, send_sem, recv_sem, hop_sem):
     n, rows, span, kv_heads, head_dim, heads = dims
     group = heads // kv_heads
     width = heads * head_dim
@@ -37,12 +37,33 @@
 
     barrier = pltpu.get_barrier_semaphore()
 
-    def greet(d, carry):
-        peer = lax.rem(me + d, n)
-        pl.semaphore_signal(barrier, inc=1, device_id=(group_id, peer), device_id_type=MESH)
-        return carry
-
-    lax.fori_loop(1, n, greet, 0)
+    chips = n // CORES
+    reach = (chips - 1) // 2
+    pairs = [(0, 1)]
+    for d in range(1, reach + 1):
+        pairs += [(d, 0), (-d, 0), (d, 1), (-d, 1)]
+    near = len(pairs)
+    if chips % 2 == 0:
+        pairs += [(chips // 2, 0), (chips // 2, 1)]
+
+    def device(offset, flip):
+        chip = lax.rem(lax.div(me, CORES) + offset + chips, chips)
+        return chip * CORES + lax.rem(lax.rem(me, CORES) + flip, CORES)
+
+    def partner(i):
+        return device(*pairs[i])
+
+    first = 1 + 4
+    for i in range(first):
+        pl.semaphore_signal(barrier, inc=1, device_id=(group_id, partner(i)), device_id_type=MESH)
+
+    def pass_on(stage):
+        for way, offset in ((0, -1), (1, 1)):
+            pl.semaphore_signal(hop_sem.at[stage, way], inc=1, device_id=(group_id, device(offset, 0)), device_id_type=MESH)
+
+    def await_stage(stage):
+        for way in range(2):
+            pl.semaphore_wait(hop_sem.at[stage, way], 1)
 
     def weight_copies(b):
         slot = ring.at[b % RING]
@@ -63,11 +84,6 @@
         for copy in weight_copies(b):
             copy.wait()
 
-    def partner(i):
-        offset, flip = pairs[i]
-        chip = lax.rem(lax.div(me, CORES) + offset + n // CORES, n // CORES)
-        return chip * CORES + lax.rem(lax.rem(me, CORES) + flip, CORES)
-
     def own_copy(c, src, land):
         return pltpu.make_async_copy(src.at[pl.ds(me * rows, rows)], land.at[:, pl.ds(me * chunk, chunk)], own_sem.at[c])
 
@@ -86,18 +102,14 @@
             send_sem=send_sem.at[c, 0], recv_sem=recv_sem.at[c, source],
             device_id=(group_id, me), device_id_type=MESH)
 
-    pl.semaphore_wait(barrier, n - 1)
-    chips = n // CORES
-    pairs = [(0, 1)]
-    for d in range(1, (chips - 1) // 2 + 1):
-        pairs += [(d, 0), (-d, 0), (d, 1), (-d, 1)]
-    near = len(pairs)
-    if chips % 2 == 0:
-        pairs += [(chips // 2, 0), (chips // 2, 1)]
-    for c, src, land, peers in ((0, k_ref, k_land, range(near)), (1, v_ref, v_land, range(near)),
-                                (0, k_ref, k_land, range(near, n - 1)), (1, v_ref, v_land, range(near, n - 1))):
+    def push_all(c, peers):
+        src, land = ((k_ref, k_land), (v_ref, v_land))[c]
         for i in peers:
             push(c, src, land, i).start()
+
+    pl.semaphore_wait(barrier, first)
+    push_all(0, range(first))
+    pass_on(2)
     own_copy(0, k_ref, k_land).start()
     own_copy(1, v_ref, v_land).start()
     small = [pltpu.make_async_copy(src, dst, small_sem.at[i]) for i, (src, dst) in enumerate((
@@ -106,6 +118,15 @@
         copy.start()
     for b in range(RING):
         start_weights(b)
+    for stage in range(2, chips // 2 + 1):
+        await_stage(stage)
+        if stage < chips // 2:
+            pass_on(stage + 1)
+        if stage <= reach:
+            push_all(0, range(1 + 4 * (stage - 1), 1 + 4 * stage))
+    push_all(1, range(near))
+    push_all(0, range(near, n - 1))
+    push_all(1, range(near, n - 1))
     for copy in small:
         copy.wait()
 
@@ -319,6 +340,7 @@
                 pltpu.SemaphoreType.DMA((2,)),
                 pltpu.SemaphoreType.DMA((2, n)),
                 pltpu.SemaphoreType.DMA((2, n)),
+                pltpu.SemaphoreType.REGULAR((n // CORES // 2 + 1, 2)),
             ],
             compiler_params=pltpu.CompilerParams(collective_id=0, has_side_effects=True, vmem_limit_bytes=8 * 1024 * 1024),
             cost_estimate=pl.CostEstimate(flops=1 << 30, bytes_accessed=1 << 27, transcendentals=0),

time: 201 us -> 205 us (1.020)
  the two profiles are of different devices: /device:TPU:53 before, /device:TPU:125 now
where the time goes in v5:
time: 205 us
  Pallas kernels  204 us (100%)
    pallas_call x1, Pallas kernels, per_device(): pl.pallas_call(functools.partial(exchange_kernel, dims), out_shape=(pltpu...  196 us
    pallas_call x1, Pallas kernels, per_device(): pl.pallas_call(functools.partial(output_kernel, 14), out_shape=(jax.Shape...  7.55 us

profile of v5, /device:TPU:125, one launch (start us, length us, event | category | flops | bytes accessed | tf_op | source)
XLA Modules:
  0.0 204.7 jit_solution(4579407627483168735)
XLA Ops:
  0.6 196.4 %shard_map.139 = (bf16[16,5120]{1,0:T(8,128)(2,1)S(1)}, bf16[2,8192,128]{2,1,0:T(8,128)(2,1)S(1)}, bf16[2,8192,128]{2,1,0:T(8,128)(2,1)S(1)}, bf16[9,512,5120]{2,1,0:T(8,128)(2,1)S(1)}) custom-call(s32[32]{0:T(128)} %lens_hbm.1, bf16[2,5120]{1,0:T(2,128)(2,1)} %x_hbm.3, bf16[5120]{0:T(1024)(128)(2,1)} %gain_hbm.1, bf16[5120]{0:T(1024)(128)(2,1)} %bq_hbm.1, ...), custom_call_target="tpu_custom_call" | custom-call | flops 1073741824 | bytes 134217728 | tf_op jit(solution)/shard_map/pallas_call | solution.py:313
  197.0 7.5 %shard_map.140 = (bf16[2,5120]{1,0:T(2,128)(2,1)}, bf16[2,8192,128]{2,1,0:T(8,128)(2,1)}, bf16[2,8192,128]{2,1,0:T(8,128)(2,1)}) custom-call(bf16[16,5120]{1,0:T(8,128)(2,1)S(1)} %get-tuple-element.10.o_ref, bf16[2,8192,128]{2,1,0:T(8,128)(2,1)S(1)} %get-tuple-element.11.k_land, bf16[2,8192,128]{2,1,0:T(8,128)(2,1)S(1)} %get-tuple-element.12.v_land, ...), custom_call_target="tpu_custom_call" | custom-call | flops 1073741824 | bytes 33554432 | tf_op jit(solution)/shard_map/pallas_call | solution.py:350

commit v6 on v4

--- a/solution.py
+++ b/solution.py
@@ -94,10 +94,16 @@
     near = len(pairs)
     if chips % 2 == 0:
         pairs += [(chips // 2, 0), (chips // 2, 1)]
-    for c, src, land, peers in ((0, k_ref, k_land, range(near)), (1, v_ref, v_land, range(near)),
-                                (0, k_ref, k_land, range(near, n - 1)), (1, v_ref, v_land, range(near, n - 1))):
-        for i in peers:
-            push(c, src, land, i).start()
+    outward = list(range(n - 1))
+    inward = [0]
+    for first in range(near, n - 1, 4):
+        inward += range(first, min(first + 4, n - 1))
+    for first in range(near - 4, 0, -4):
+        inward += range(first, first + 4)
+    for i in outward:
+        push(0, k_ref, k_land, i).start()
+    for i in inward:
+        push(1, v_ref, v_land, i).start()
     own_copy(0, k_ref, k_land).start()
     own_copy(1, v_ref, v_land).start()
     small = [pltpu.make_async_copy(src, dst, small_sem.at[i]) for i, (src, dst) in enumerate((
@@ -212,7 +218,7 @@
 
     own_copy(0, k_ref, k_land).wait()
     score_chunk(me)
-    for i in range(n - 1):
+    for i in outward:
         source = partner(i)
         arrival(0, k_land, source).wait_recv()
         score_chunk(source)
@@ -220,7 +226,7 @@
         m_acc[s] = jnp.broadcast_to(jnp.max(m_acc[s], axis=-1, keepdims=True), (heads, head_dim))
     own_copy(1, v_ref, v_land).wait()
     value_chunk(me)
-    for i in range(n - 1):
+    for i in inward:
         source = partner(i)
         arrival(1, v_land, source).wait_recv()
         value_chunk(source)

time: 201 us -> 204 us (1.015); the launches traced: 201 us -> 201 us
  no operation moved by 1% of the time
where the time goes in v6:
time: 204 us; the launch traced here: 201 us
  Pallas kernels  200 us (98%)
    pallas_call x1, Pallas kernels, per_device(): pl.pallas_call(functools.partial(exchange_kernel, dims), out_shape=(pltpu...  193 us
    pallas_call x1, Pallas kernels, per_device(): pl.pallas_call(functools.partial(output_kernel, 14), out_shape=(jax.Shape...  7.55 us

profile of v6, /device:TPU:53, one launch (start us, length us, event | category | flops | bytes accessed | tf_op | source)
XLA Modules:
  0.0 201.1 jit_solution(13833934696344833087)
XLA Ops:
  0.6 192.9 %shard_map.139 = (bf16[16,5120]{1,0:T(8,128)(2,1)S(1)}, bf16[2,8192,128]{2,1,0:T(8,128)(2,1)S(1)}, bf16[2,8192,128]{2,1,0:T(8,128)(2,1)S(1)}, bf16[9,512,5120]{2,1,0:T(8,128)(2,1)S(1)}) custom-call(s32[32]{0:T(128)} %lens_hbm.1, bf16[2,5120]{1,0:T(2,128)(2,1)} %x_hbm.3, bf16[5120]{0:T(1024)(128)(2,1)} %gain_hbm.1, bf16[5120]{0:T(1024)(128)(2,1)} %bq_hbm.1, ...), custom_call_target="tpu_custom_call" | custom-call | flops 1073741824 | bytes 134217728 | tf_op jit(solution)/shard_map/pallas_call | solution.py:298
  193.6 7.5 %shard_map.140 = (bf16[2,5120]{1,0:T(2,128)(2,1)}, bf16[2,8192,128]{2,1,0:T(8,128)(2,1)}, bf16[2,8192,128]{2,1,0:T(8,128)(2,1)}) custom-call(bf16[16,5120]{1,0:T(8,128)(2,1)S(1)} %get-tuple-element.10.o_ref, bf16[2,8192,128]{2,1,0:T(8,128)(2,1)S(1)} %get-tuple-element.11.k_land, bf16[2,8192,128]{2,1,0:T(8,128)(2,1)S(1)} %get-tuple-element.12.v_land, ...), custom_call_target="tpu_custom_call" | custom-call | flops 1073741824 | bytes 33554432 | tf_op jit(solution)/shard_map/pallas_call | solution.py:334

commit v7 on v5

--- a/solution.py
+++ b/solution.py
@@ -101,6 +101,11 @@
             dst_ref=land.at[:, pl.ds(source * chunk, chunk)],
             send_sem=send_sem.at[c, 0], recv_sem=recv_sem.at[c, source],
             device_id=(group_id, me), device_id_type=MESH)
+
+    outward = list(range(n - 1))
+    inward = [0] + outward[near:]
+    for d in range(reach, 0, -1):
+        inward += range(1 + 4 * (d - 1), 1 + 4 * d)
 
     def push_all(c, peers):
         src, land = ((k_ref, k_land), (v_ref, v_land))[c]
@@ -124,9 +129,8 @@
             pass_on(stage + 1)
         if stage <= reach:
             push_all(0, range(1 + 4 * (stage - 1), 1 + 4 * stage))
-    push_all(1, range(near))
-    push_all(0, range(near, n - 1))
-    push_all(1, range(near, n - 1))
+    push_all(0, outward[near:])
+    push_all(1, inward)
     for copy in small:
         copy.wait()
 
@@ -233,7 +237,7 @@
 
     own_copy(0, k_ref, k_land).wait()
     score_chunk(me)
-    for i in range(n - 1):
+    for i in outward:
         source = partner(i)
         arrival(0, k_land, source).wait_recv()
         score_chunk(source)
@@ -241,7 +245,7 @@
         m_acc[s] = jnp.broadcast_to(jnp.max(m_acc[s], axis=-1, keepdims=True), (heads, head_dim))
     own_copy(1, v_ref, v_land).wait()
     value_chunk(me)
-    for i in range(n - 1):
+    for i in inward:
         source = partner(i)
         arrival(1, v_land, source).wait_recv()
         value_chunk(source)

time: 205 us -> 205 us (level)
  the two profiles are of different devices: /device:TPU:125 before, /device:TPU:53 now
where the time goes in v7:
time: 205 us; the launch traced here: 202 us
  Pallas kernels  201 us (98%)
    pallas_call x1, Pallas kernels, per_device(): pl.pallas_call(functools.partial(exchange_kernel, dims), out_shape=(pltpu...  193 us
    pallas_call x1, Pallas kernels, per_device(): pl.pallas_call(functools.partial(output_kernel, 14), out_shape=(jax.Shape...  7.55 us

profile of v7, /device:TPU:53, one launch (start us, length us, event | category | flops | bytes accessed | tf_op | source)
XLA Modules:
  0.0 201.7 jit_solution(2794754268275640531)
XLA Ops:
  0.6 193.4 %shard_map.139 = (bf16[16,5120]{1,0:T(8,128)(2,1)S(1)}, bf16[2,8192,128]{2,1,0:T(8,128)(2,1)S(1)}, bf16[2,8192,128]{2,1,0:T(8,128)(2,1)S(1)}, bf16[9,512,5120]{2,1,0:T(8,128)(2,1)S(1)}) custom-call(s32[32]{0:T(128)} %lens_hbm.1, bf16[2,5120]{1,0:T(2,128)(2,1)} %x_hbm.3, bf16[5120]{0:T(1024)(128)(2,1)} %gain_hbm.1, bf16[5120]{0:T(1024)(128)(2,1)} %bq_hbm.1, ...), custom_call_target="tpu_custom_call" | custom-call | flops 1073741824 | bytes 134217728 | tf_op jit(solution)/shard_map/pallas_call | solution.py:317
  194.0 7.5 %shard_map.140 = (bf16[2,5120]{1,0:T(2,128)(2,1)}, bf16[2,8192,128]{2,1,0:T(8,128)(2,1)}, bf16[2,8192,128]{2,1,0:T(8,128)(2,1)}) custom-call(bf16[16,5120]{1,0:T(8,128)(2,1)S(1)} %get-tuple-element.10.o_ref, bf16[2,8192,128]{2,1,0:T(8,128)(2,1)S(1)} %get-tuple-element.11.k_land, bf16[2,8192,128]{2,1,0:T(8,128)(2,1)S(1)} %get-tuple-element.12.v_land, ...), custom_call_target="tpu_custom_call" | custom-call | flops 1073741824 | bytes 33554432 | tf_op jit(solution)/shard_map/pallas_call | solution.py:354

commit v8 on v4

--- a/solution.py
+++ b/solution.py
@@ -71,19 +71,30 @@
     def own_copy(c, src, land):
         return pltpu.make_async_copy(src.at[pl.ds(me * rows, rows)], land.at[:, pl.ds(me * chunk, chunk)], own_sem.at[c])
 
-    def push(c, src, land, i):
+    sides = ((k_ref, k_land), (v_ref, v_land))
+
+    def seqs(part):
+        return pl.ds(0, rows) if part is None else pl.ds(part, 1)
+
+    def push(c, i, part=None):
+        src, land = sides[c]
         peer = partner(i)
+        lane = 0 if part is None else part
+        first, count = (peer * rows, rows) if part is None else (peer * rows + part, 1)
         return pltpu.make_async_remote_copy(
-            src_ref=src.at[pl.ds(peer * rows, rows)],
-            dst_ref=land.at[:, pl.ds(me * chunk, chunk)],
-            send_sem=send_sem.at[c, i], recv_sem=recv_sem.at[c, me],
+            src_ref=src.at[pl.ds(first, count)],
+            dst_ref=land.at[seqs(part), pl.ds(me * chunk, chunk)],
+            send_sem=send_sem.at[lane, c, i], recv_sem=recv_sem.at[lane, c, me],
             device_id=(group_id, peer), device_id_type=MESH)
 
-    def arrival(c, land, source):
+    def arrival(c, i, part=None):
+        land = sides[c][1]
+        source = partner(i)
+        lane = 0 if part is None else part
+        place = land.at[seqs(part), pl.ds(source * chunk, chunk)]
         return pltpu.make_async_remote_copy(
-            src_ref=land.at[:, pl.ds(source * chunk, chunk)],
-            dst_ref=land.at[:, pl.ds(source * chunk, chunk)],
-            send_sem=send_sem.at[c, 0], recv_sem=recv_sem.at[c, source],
+            src_ref=place, dst_ref=place,
+            send_sem=send_sem.at[lane, c, i], recv_sem=recv_sem.at[lane, c, source],
             device_id=(group_id, me), device_id_type=MESH)
 
     pl.semaphore_wait(barrier, n - 1)
@@ -94,10 +105,25 @@
     near = len(pairs)
     if chips % 2 == 0:
         pairs += [(chips // 2, 0), (chips // 2, 1)]
-    for c, src, land, peers in ((0, k_ref, k_land, range(near)), (1, v_ref, v_land, range(near)),
-                                (0, k_ref, k_land, range(near, n - 1)), (1, v_ref, v_land, range(near, n - 1))):
-        for i in peers:
-            push(c, src, land, i).start()
+    cut = ((1, 2), (1, 2, near))
+    halves = tuple(range(rows))
+
+    def parts(c, i):
+        return halves if i in cut[c] else (None,)
+
+    stretches = []
+    for todo in ([(0, i) for i in range(near)], [(1, i) for i in range(near)],
+                 [(0, i) for i in range(near, n - 1)] + [(1, i) for i in range(near, n - 1)]):
+        even = [(c, i, part) for c, i in todo for part in parts(c, i)]
+        odd = [e for e in even if e[2] in (None, 0)] + [e for e in even if e[2] not in (None, 0)]
+        stretches.append((even, odd))
+    core = lax.rem(me, CORES)
+    for which in range(CORES):
+        @pl.when(core == which)
+        def _():
+            for stretch in stretches:
+                for c, i, part in stretch[which]:
+                    push(c, i, part).start()
     own_copy(0, k_ref, k_land).start()
     own_copy(1, v_ref, v_land).start()
     small = [pltpu.make_async_copy(src, dst, small_sem.at[i]) for i, (src, dst) in enumerate((
@@ -214,7 +240,8 @@
     score_chunk(me)
     for i in range(n - 1):
         source = partner(i)
-        arrival(0, k_land, source).wait_recv()
+        for part in parts(0, i):
+            arrival(0, i, part).wait_recv()
         score_chunk(source)
     for s in range(rows):
         m_acc[s] = jnp.broadcast_to(jnp.max(m_acc[s], axis=-1, keepdims=True), (heads, head_dim))
@@ -222,7 +249,8 @@
     value_chunk(me)
     for i in range(n - 1):
         source = partner(i)
-        arrival(1, v_land, source).wait_recv()
+        for part in parts(1, i):
+            arrival(1, i, part).wait_recv()
         value_chunk(source)
 
     o_row[...] = jnp.zeros_like(o_row)
@@ -234,9 +262,10 @@
     o_ref[...] = o_row[...].astype(jnp.bfloat16)
     for b in range(14, 14 + RING):
         wait_weights(b)
-    for c, (src, land) in enumerate(((k_ref, k_land), (v_ref, v_land))):
+    for c in range(2):
         for i in range(n - 1):
-            push(c, src, land, i).wait_send()
+            for part in parts(c, i):
+                push(c, i, part).wait_send()
 
 
 def output_kernel(first, o_ref, k_land, v_land, ring, x_hbm, wo_ref, y_ref, k_out, v_out, x_ref, extra, acc, sem):
@@ -317,8 +346,8 @@
                 pltpu.SemaphoreType.DMA((6,)),
                 pltpu.SemaphoreType.DMA((RING, PACK)),
                 pltpu.SemaphoreType.DMA((2,)),
-                pltpu.SemaphoreType.DMA((2, n)),
-                pltpu.SemaphoreType.DMA((2, n)),
+                pltpu.SemaphoreType.DMA((rows, 2, n)),
+                pltpu.SemaphoreType.DMA((rows, 2, n)),
             ],
             compiler_params=pltpu.CompilerParams(collective_id=0, has_side_effects=True, vmem_limit_bytes=8 * 1024 * 1024),
             cost_estimate=pl.CostEstimate(flops=1 << 30, bytes_accessed=1 << 27, transcendentals=0),

time: 201 us -> 202 us (level)
  no operation moved by 1% of the time
where the time goes in v8:
time: 202 us
  Pallas kernels  201 us (100%)
    pallas_call x1, Pallas kernels, per_device(): pl.pallas_call(functools.partial(exchange_kernel, dims), out_shape=(pltpu...  194 us
    pallas_call x1, Pallas kernels, per_device(): pl.pallas_call(functools.partial(output_kernel, 14), out_shape=(jax.Shape...  7.55 us

profile of v8, /device:TPU:53, one launch (start us, length us, event | category | flops | bytes accessed | tf_op | source)
XLA Modules:
  0.0 202.0 jit_solution(17225735032755815327)
XLA Ops:
  0.6 193.6 %shard_map.139 = (bf16[16,5120]{1,0:T(8,128)(2,1)S(1)}, bf16[2,8192,128]{2,1,0:T(8,128)(2,1)S(1)}, bf16[2,8192,128]{2,1,0:T(8,128)(2,1)S(1)}, bf16[9,512,5120]{2,1,0:T(8,128)(2,1)S(1)}) custom-call(s32[32]{0:T(128)} %lens_hbm.1, bf16[2,5120]{1,0:T(2,128)(2,1)} %x_hbm.3, bf16[5120]{0:T(1024)(128)(2,1)} %gain_hbm.1, bf16[5120]{0:T(1024)(128)(2,1)} %bq_hbm.1, ...), custom_call_target="tpu_custom_call" | custom-call | flops 1073741824 | bytes 134217728 | tf_op jit(solution)/shard_map/pallas_call | solution.py:321
  194.3 7.5 %shard_map.140 = (bf16[2,5120]{1,0:T(2,128)(2,1)}, bf16[2,8192,128]{2,1,0:T(8,128)(2,1)}, bf16[2,8192,128]{2,1,0:T(8,128)(2,1)}) custom-call(bf16[16,5120]{1,0:T(8,128)(2,1)S(1)} %get-tuple-element.10.o_ref, bf16[2,8192,128]{2,1,0:T(8,128)(2,1)S(1)} %get-tuple-element.11.k_land, bf16[2,8192,128]{2,1,0:T(8,128)(2,1)S(1)} %get-tuple-element.12.v_land, ...), custom_call_target="tpu_custom_call" | custom-call | flops 1073741824 | bytes 33554432 | tf_op jit(solution)/shard_map/pallas_call | solution.py:357

commit v9 on v4

--- a/solution.py
+++ b/solution.py
@@ -10,7 +10,7 @@
 RMS_EPS = 1e-6
 ROPE_THETA = 1000000.0
 MASKED = -1e30
-RING = 9
+RING = 8
 PACK = 5
 TILE = 512
 OUT_TILE = 512
@@ -19,11 +19,19 @@
 MESH = pl.DeviceIdType.MESH
 
 
+def multiply_block(o_ref, r, weights, out):
+    block, width = weights.shape
+    lhs = o_ref[:, r * block:(r + 1) * block]
+    for t in range(width // OUT_TILE):
+        cols = slice(t * OUT_TILE, (t + 1) * OUT_TILE)
+        out[:, cols] += jnp.dot(lhs, weights[:, cols], preferred_element_type=jnp.float32)
+
+
 def exchange_kernel(dims, lens_hbm, x_hbm, gain_hbm, bq_hbm, bk_hbm, bv_hbm, k_ref, v_ref, wq_ref, wk_ref, wv_ref, wo_ref,
-                    o_ref, k_land, v_land, ring,
+                    o_ref, k_land, v_land, ring, y_part,
                     lens_ref, x_ref, gain_ref, bq_ref, bk_ref, bv_ref,
                     scores, h_ref, acc, acc_kv, q_raw, q_rot, k_raw, v_raw, o_acc, m_acc, l_acc, o_row,
-                    small_sem, ring_sem, own_sem, send_sem, recv_sem):
+                    staged, packed, half_land, small_sem, ring_sem, own_sem, send_sem, recv_sem, stage_sem, half_send, half_recv):
     n, rows, span, kv_heads, head_dim, heads = dims
     group = heads // kv_heads
     width = heads * head_dim
@@ -95,11 +103,25 @@
     if chips % 2 == 0:
         pairs += [(chips // 2, 0), (chips // 2, 1)]
     for c, src, land, peers in ((0, k_ref, k_land, range(near)), (1, v_ref, v_land, range(near)),
-                                (0, k_ref, k_land, range(near, n - 1)), (1, v_ref, v_land, range(near, n - 1))):
+                                (0, k_ref, k_land, range(near, n - 1))):
         for i in peers:
             push(c, src, land, i).start()
     own_copy(0, k_ref, k_land).start()
     own_copy(1, v_ref, v_land).start()
+
+    last = range(n - 1 - near)
+
+    def stage_copy(f):
+        return pltpu.make_async_copy(v_ref.at[pl.ds(partner(near + f) * rows, rows)], staged.at[f], stage_sem.at[f])
+
+    def push_half(part, f):
+        return pltpu.make_async_remote_copy(
+            src_ref=packed.at[part, f], dst_ref=half_land.at[part, f],
+            send_sem=half_send.at[part, f], recv_sem=half_recv.at[part, f],
+            device_id=(group_id, partner(near + f)), device_id_type=MESH)
+
+    for f in last:
+        stage_copy(f).start()
     small = [pltpu.make_async_copy(src, dst, small_sem.at[i]) for i, (src, dst) in enumerate((
         (lens_hbm, lens_ref), (x_hbm, x_ref), (gain_hbm, gain_ref), (bq_hbm, bq_ref), (bk_hbm, bk_ref), (bv_hbm, bv_ref)))]
     for copy in small:
@@ -136,6 +158,17 @@
             return carry
         lax.fori_loop(0, PACK, part, 0)
 
+    half = kv_heads // 2
+    tile_row = lax.broadcasted_iota(jnp.int32, (span // 2, kv_heads, head_dim), 1)
+    for f in last:
+        stage_copy(f).wait()
+        for s in range(rows):
+            pair = staged[f, s].astype(jnp.float32).reshape(span // 2, 2, kv_heads, head_dim)
+            even, odd = pair[:, 0], pair[:, 1]
+            for part, both in enumerate((jnp.where(tile_row < half, even, pltpu.roll(odd, half, 1)),
+                                         jnp.where(tile_row < half, pltpu.roll(even, half, 1), odd))):
+                packed[part, f, s] = both.reshape(chunk // 2, head_dim).astype(jnp.bfloat16)
+
     for b in range(4):
         wait_weights(b)
         multiply_kv(b)
@@ -145,6 +178,10 @@
         multiply(h_ref[:, pl.ds((b - 4) * block, block)], b % RING, acc, width // TILE)
         if b + RING < 14 + RING:
             start_weights(b + RING)
+
+    for part in range(2):
+        for f in last:
+            push_half(part, f).start()
 
     lane = lax.broadcasted_iota(jnp.int32, (1, head_dim), 1)
     freq_idx = jnp.where(lane < half_dim, lane, lane - half_dim).astype(jnp.float32)
@@ -199,12 +236,51 @@
             scores[s, :, place] = sc
             m_acc[s] = jnp.maximum(m_acc[s], lane_fold(jnp.maximum, sc))
 
+    head_row = lax.broadcasted_iota(jnp.int32, (span, kv_heads, head_dim), 1)
+
+    def settle_half(s, f, source, part):
+        place = pl.ds(pl.multiple_of(source * chunk, chunk), chunk)
+        limit = lens_ref[me * rows + s] - source * span
+        both = half_land[part, f, s].astype(jnp.float32).reshape(span // 2, kv_heads, head_dim)
+        turned = pltpu.roll(both, half, 1)
+        even, odd = (both, turned) if part == 0 else (turned, both)
+        old = jnp.stack([even, odd], axis=1).reshape(span, kv_heads, head_dim)
+        kept = jnp.where(row_idx < limit, old, jnp.where(row_idx == limit, v_raw[s][None], 0.0))
+        mine = head_row < half if part == 0 else head_row >= half
+        kept = jnp.where(mine, kept, 0.0)
+        full = kept
+        if part:
+            full = jnp.where(mine, kept, v_land[s, place, :].astype(jnp.float32).reshape(span, kv_heads, head_dim))
+        v_land[s, place, :] = full.reshape(chunk, head_dim).astype(jnp.bfloat16)
+        return kept.reshape(chunk, head_dim).astype(jnp.bfloat16), place
+
+    def weigh(s, place, vals, count):
+        e = jnp.exp(scores[s, :, place] - m_acc[s][:, :1])
+        if count:
+            l_acc[s] += lane_fold(jnp.add, e)
+        o_acc[s] += jnp.dot(e.astype(jnp.bfloat16), vals, preferred_element_type=jnp.float32)
+
     def value_chunk(source):
         for s in range(rows):
-            vals, place, limit = settle(v_land, s, source, v_raw)
-            e = jnp.exp(scores[s, :, place] - m_acc[s][:, :1])
-            l_acc[s] += lane_fold(jnp.add, e)
-            o_acc[s] += jnp.dot(e.astype(jnp.bfloat16), vals, preferred_element_type=jnp.float32)
+            vals, place, _ = settle(v_land, s, source, v_raw)
+            weigh(s, place, vals, True)
+
+    def value_half(part):
+        for f in last:
+            push_half(part, f).wait_recv()
+            for s in range(rows):
+                vals, place = settle_half(s, f, partner(near + f), part)
+                weigh(s, place, vals, part == 0)
+
+    def finish_heads(part):
+        start, stop = part * heads // 2, (part + 1) * heads // 2
+        for s in range(rows):
+            l_all = jnp.sum(l_acc[s, pl.ds(start, stop - start), :], axis=-1, keepdims=True)
+            q_raw[s, pl.ds(start, stop - start), :] = o_acc[s, pl.ds(start, stop - start), :] / l_all
+            for j in range(start, stop):
+                o_row[pl.ds(s, 1), j * head_dim:(j + 1) * head_dim] = q_raw[s, pl.ds(j, 1), :]
+        cols = slice(start * head_dim, stop * head_dim)
+        o_ref[:, cols] = o_row[:, cols].astype(jnp.bfloat16)
 
     m_acc[...] = jnp.full_like(m_acc, MASKED)
     l_acc[...] = jnp.zeros_like(l_acc)
@@ -220,51 +296,43 @@
         m_acc[s] = jnp.broadcast_to(jnp.max(m_acc[s], axis=-1, keepdims=True), (heads, head_dim))
     own_copy(1, v_ref, v_land).wait()
     value_chunk(me)
-    for i in range(n - 1):
+    for i in range(near):
         source = partner(i)
         arrival(1, v_land, source).wait_recv()
         value_chunk(source)
-
     o_row[...] = jnp.zeros_like(o_row)
-    for s in range(rows):
-        l_all = jnp.sum(l_acc[s], axis=-1, keepdims=True)
-        q_raw[s] = o_acc[s] / l_all
-        for j in range(heads):
-            o_row[pl.ds(s, 1), j * head_dim:(j + 1) * head_dim] = q_raw[s, pl.ds(j, 1), :]
-    o_ref[...] = o_row[...].astype(jnp.bfloat16)
-    for b in range(14, 14 + RING):
-        wait_weights(b)
+    y_part[...] = jnp.zeros_like(y_part)
+    value_half(0)
+    finish_heads(0)
+    for r in range(depth // block // 2):
+        wait_weights(14 + r)
+        multiply_block(o_ref, r, ring.at[(14 + r) % RING], y_part)
+        if 14 + r + RING < 24:
+            start_weights(14 + r + RING)
+    value_half(1)
+    finish_heads(1)
+    for r in range(depth // block // 2, depth // block):
+        wait_weights(14 + r)
     for c, (src, land) in enumerate(((k_ref, k_land), (v_ref, v_land))):
-        for i in range(n - 1):
+        for i in range(n - 1 if c == 0 else near):
             push(c, src, land, i).wait_send()
-
-
-def output_kernel(first, o_ref, k_land, v_land, ring, x_hbm, wo_ref, y_ref, k_out, v_out, x_ref, extra, acc, sem):
+    for part in range(2):
+        for f in last:
+            push_half(part, f).wait_send()
+
+
+def output_kernel(first, start, o_ref, k_land, v_land, ring, y_part, x_hbm, y_ref, k_out, v_out, x_ref, acc, sem):
     rows, depth = x_ref.shape
-    block, width = extra.shape[1:]
-    resident = ring.shape[0]
-    tail = [pltpu.make_async_copy(wo_ref.at[pl.ds((resident + i) * block, block)], extra.at[i], sem.at[i])
-            for i in range(extra.shape[0])]
-    rest = [pltpu.make_async_copy(x_hbm, x_ref, sem.at[len(tail)]),
-            pltpu.make_async_copy(k_land, k_out, sem.at[len(tail) + 1]),
-            pltpu.make_async_copy(v_land, v_out, sem.at[len(tail) + 2])]
-    for copy in tail + rest:
+    block = ring.shape[1]
+    copies = [pltpu.make_async_copy(k_land, k_out, sem.at[0]),
+              pltpu.make_async_copy(v_land, v_out, sem.at[1]),
+              pltpu.make_async_copy(x_hbm, x_ref, sem.at[2])]
+    for copy in copies:
         copy.start()
-    acc[...] = jnp.zeros_like(acc)
-
-    def multiply(r, weights):
-        lhs = o_ref[:, r * block:(r + 1) * block]
-
-        for t in range(width // OUT_TILE):
-            cols = slice(t * OUT_TILE, (t + 1) * OUT_TILE)
-            acc[:, cols] += jnp.dot(lhs, weights[:, cols], preferred_element_type=jnp.float32)
-
-    for r in range(resident):
-        multiply(r, ring.at[(first + r) % resident])
-    for i, copy in enumerate(tail):
-        copy.wait()
-        multiply(resident + i, extra.at[i])
-    for copy in rest:
+    acc[...] = y_part[...]
+    for r in range(start, depth // block):
+        multiply_block(o_ref, r, ring.at[(first + r) % ring.shape[0]], acc)
+    for copy in copies:
         copy.wait()
     y_ref[...] = (x_ref[...].astype(jnp.float32) + acc[:rows, :]).astype(jnp.bfloat16)
 
@@ -289,12 +357,12 @@
         hbm = pl.BlockSpec(memory_space=pl.ANY)
         bf16, f32 = jnp.bfloat16, jnp.float32
         land = (rows, n * chunk, head_dim)
-        o_rows, k_all, v_all, ring = pl.pallas_call(
+        o_rows, k_all, v_all, ring, y_part = pl.pallas_call(
             functools.partial(exchange_kernel, dims),
             out_shape=(pltpu.VMEM((LHS_ROWS, width), bf16), pltpu.VMEM(land, bf16), pltpu.VMEM(land, bf16),
-                       pltpu.VMEM((RING, block, width), bf16)),
+                       pltpu.VMEM((RING, block, width), bf16), pltpu.VMEM((LHS_ROWS, depth), f32)),
             in_specs=[hbm] * 12,
-            out_specs=(vmem,) * 4,
+            out_specs=(vmem,) * 5,
             scratch_shapes=[
                 pltpu.SMEM((batch,), jnp.int32),
                 pltpu.VMEM((rows, depth), bf16),
@@ -314,31 +382,35 @@
                 pltpu.VMEM((rows, heads, head_dim), f32),
                 pltpu.VMEM((rows, heads, head_dim), f32),
                 pltpu.VMEM((LHS_ROWS, width), f32),
+                pltpu.VMEM((CORES, rows, chunk, head_dim), bf16),
+                pltpu.VMEM((2, CORES, rows, chunk // 2, head_dim), bf16),
+                pltpu.VMEM((2, CORES, rows, chunk // 2, head_dim), bf16),
                 pltpu.SemaphoreType.DMA((6,)),
                 pltpu.SemaphoreType.DMA((RING, PACK)),
                 pltpu.SemaphoreType.DMA((2,)),
                 pltpu.SemaphoreType.DMA((2, n)),
                 pltpu.SemaphoreType.DMA((2, n)),
+                pltpu.SemaphoreType.DMA((CORES,)),
+                pltpu.SemaphoreType.DMA((2, CORES)),
+                pltpu.SemaphoreType.DMA((2, CORES)),
             ],
             compiler_params=pltpu.CompilerParams(collective_id=0, has_side_effects=True, vmem_limit_bytes=8 * 1024 * 1024),
             cost_estimate=pl.CostEstimate(flops=1 << 30, bytes_accessed=1 << 27, transcendentals=0),
         )(prompt_lens, x_tok, norm_gain, b_q, b_k, b_v,
           k_cache.reshape(batch, chunk, head_dim), v_cache.reshape(batch, chunk, head_dim), w_q, w_k, w_v, w_o)
-        extra = depth // block - RING
         y, k_out, v_out = pl.pallas_call(
-            functools.partial(output_kernel, 14),
+            functools.partial(output_kernel, 14, depth // block // 2),
             out_shape=(jax.ShapeDtypeStruct((rows, depth), bf16), jax.ShapeDtypeStruct(land, bf16), jax.ShapeDtypeStruct(land, bf16)),
-            in_specs=[vmem] * 4 + [hbm] * 2,
+            in_specs=[vmem] * 5 + [hbm],
             out_specs=(vmem, hbm, hbm),
             scratch_shapes=[
                 pltpu.VMEM((rows, depth), bf16),
-                pltpu.VMEM((extra, block, width), bf16),
                 pltpu.VMEM((LHS_ROWS, depth), f32),
-                pltpu.SemaphoreType.DMA((extra + 3,)),
+                pltpu.SemaphoreType.DMA((3,)),
             ],
-            compiler_params=pltpu.CompilerParams(vmem_limit_bytes=(extra * 6 + 2) * 1024 * 1024),
+            compiler_params=pltpu.CompilerParams(vmem_limit_bytes=3 * 1024 * 1024),
             cost_estimate=pl.CostEstimate(flops=1 << 30, bytes_accessed=1 << 25, transcendentals=0),
-        )(*[pltpu.with_memory_space_constraint(a, pltpu.VMEM) for a in (o_rows, k_all, v_all, ring)], x_tok, w_o)
+        )(*[pltpu.with_memory_space_constraint(a, pltpu.VMEM) for a in (o_rows, k_all, v_all, ring, y_part)], x_tok)
         shape = (rows, n * span, kv_heads, head_dim)
         return y, k_out.reshape(shape), v_out.reshape(shape)
 

time: 201 us -> 234 us (1.16)
  local copies, waits for them, and re-layouts: 0 us -> 31 us
    unnamed x0 -> x10, local copies, waits for them, and re-layouts: none -> 31 us
    pallas_call x1, Pallas kernels: 193 us -> 198 us  [per_device(): pl.pallas_call(functools.partial(exchange_kernel, dims), out_shape=(pltpu...]
    pallas_call x1, Pallas kernels: 7.55 us -> 4.17 us  [per_device(): pl.pallas_call(functools.partial(output_kernel, 14, depth // block // 2),...]
where the time goes in v9:
time: 234 us
  Pallas kernels  202 us (86%)
  local copies, waits for them, and re-layouts  31 us (13%)
    pallas_call x1, Pallas kernels, per_device(): pl.pallas_call(functools.partial(exchange_kernel, dims), out_shape=(pltpu...  198 us
    unnamed x10, local copies, waits for them, and re-layouts  31 us

profile of v9, /device:TPU:53, one launch (start us, length us, event | category | flops | bytes accessed | tf_op | source)
XLA Modules:
  0.0 234.0 jit_solution(4111904603297393509)
XLA Ops:
  0.6 0.0 copy-start.4
  0.6 198.0 %shard_map.139 = (bf16[16,5120]{1,0:T(8,128)(2,1)S(1)}, bf16[2,8192,128]{2,1,0:T(8,128)(2,1)S(1)}, bf16[2,8192,128]{2,1,0:T(8,128)(2,1)S(1)}, bf16[8,512,5120]{2,1,0:T(8,128)(2,1)S(1)}, f32[16,5120]{1,0:T(8,128)S(1)}) custom-call(s32[32]{0:T(128)} %lens_hbm.1, bf16[2,5120]{1,0:T(2,128)(2,1)} %x_hbm.3, bf16[5120]{0:T(1024)(128)(2,1)} %gain_hbm.1, ...), custom_call_target="tpu_custom_call" | custom-call | flops 1073741824 | bytes 134217728 | tf_op jit(solution)/shard_map/pallas_call | solution.py:360
  198.7 0.0 copy-start
  198.7 13.8 %copy-done = bf16[8,512,5120]{2,1,0:T(8,128)(2,1)} copy-done((bf16[8,512,5120]{2,1,0:T(8,128)(2,1)}, bf16[8,512,5120]{2,1,0:T(8,128)(2,1)S(1)}, u32[]{:S(2)}) %copy-start) | copy-done | bytes 41943064
  212.5 0.0 copy-start.2
  212.5 2.0 copy-done.2
  214.5 0.0 copy-done.4
  214.5 0.0 copy-start.1
  214.5 13.0 %copy-done.1 = bf16[8,512,5120]{2,1,0:T(8,128)(2,1)S(1)} copy-done((bf16[8,512,5120]{2,1,0:T(8,128)(2,1)S(1)}, bf16[8,512,5120]{2,1,0:T(8,128)(2,1)}, u32[]{:S(2)}) %copy-start.1) | copy-done | bytes 41943064
  227.5 0.0 copy-start.3
  227.5 2.2 copy-done.3
  229.7 4.2 %shard_map.140 = (bf16[2,5120]{1,0:T(2,128)(2,1)}, bf16[2,8192,128]{2,1,0:T(8,128)(2,1)}, bf16[2,8192,128]{2,1,0:T(8,128)(2,1)}) custom-call(bf16[16,5120]{1,0:T(8,128)(2,1)S(1)} %get-tuple-element.11.o_ref, bf16[2,8192,128]{2,1,0:T(8,128)(2,1)S(1)} %get-tuple-element.12.k_land, bf16[2,8192,128]{2,1,0:T(8,128)(2,1)S(1)} %copy-done.3, ...), custom_call_target="tpu_custom_call" | custom-call | flops 1073741824 | bytes 33554432 | tf_op jit(solution)/shard_map/pallas_call | solution.py:401
Async XLA Ops:
  0.6 213.9 %copy-start.4 = (bf16[2,5120]{1,0:T(2,128)(2,1)S(1)}, bf16[2,5120]{1,0:T(2,128)(2,1)}, u32[]{:S(2)}) copy-start(bf16[2,5120]{1,0:T(2,128)(2,1)} %x_hbm.3) | copy-start | bytes 61444
  198.7 13.8 %copy-start = (bf16[8,512,5120]{2,1,0:T(8,128)(2,1)}, bf16[8,512,5120]{2,1,0:T(8,128)(2,1)S(1)}, u32[]{:S(2)}) copy-start(bf16[8,512,5120]{2,1,0:T(8,128)(2,1)S(1)} %get-tuple-element.14.ring) | copy-start | bytes 125829120
  212.5 2.0 copy-start.2
  214.5 13.0 %copy-start.1 = (bf16[8,512,5120]{2,1,0:T(8,128)(2,1)S(1)}, bf16[8,512,5120]{2,1,0:T(8,128)(2,1)}, u32[]{:S(2)}) copy-start(bf16[8,512,5120]{2,1,0:T(8,128)(2,1)} %copy-done) | copy-start | bytes 125829120
  227.5 2.2 copy-start.3

commit v10 on v9

--- a/solution.py
+++ b/solution.py
@@ -408,7 +408,7 @@
                 pltpu.VMEM((LHS_ROWS, depth), f32),
                 pltpu.SemaphoreType.DMA((3,)),
             ],
-            compiler_params=pltpu.CompilerParams(vmem_limit_bytes=3 * 1024 * 1024),
+            compiler_params=pltpu.CompilerParams(vmem_limit_bytes=8 * 1024 * 1024),
             cost_estimate=pl.CostEstimate(flops=1 << 30, bytes_accessed=1 << 25, transcendentals=0),
         )(*[pltpu.with_memory_space_constraint(a, pltpu.VMEM) for a in (o_rows, k_all, v_all, ring, y_part)], x_tok)
         shape = (rows, n * span, kv_heads, head_dim)

time: 234 us -> 203 us (0.87)
  local copies, waits for them, and re-layouts: 31 us -> 0 us
    unnamed x10 -> x0, local copies, waits for them, and re-layouts: 31 us -> none
where the time goes in v10:
time: 203 us
  Pallas kernels  202 us (100%)
    pallas_call x1, Pallas kernels, per_device(): pl.pallas_call(functools.partial(exchange_kernel, dims), out_shape=(pltpu...  198 us
    pallas_call x1, Pallas kernels, per_device(): pl.pallas_call(functools.partial(output_kernel, 14, depth // block // 2),...  4.16 us

profile of v10, /device:TPU:53, one launch (start us, length us, event | category | flops | bytes accessed | tf_op | source)
XLA Modules:
  0.0 203.0 jit_solution(13330251181338958558)
XLA Ops:
  0.6 198.0 %shard_map.139 = (bf16[16,5120]{1,0:T(8,128)(2,1)S(1)}, bf16[2,8192,128]{2,1,0:T(8,128)(2,1)S(1)}, bf16[2,8192,128]{2,1,0:T(8,128)(2,1)S(1)}, bf16[8,512,5120]{2,1,0:T(8,128)(2,1)S(1)}, f32[16,5120]{1,0:T(8,128)S(1)}) custom-call(s32[32]{0:T(128)} %lens_hbm.1, bf16[2,5120]{1,0:T(2,128)(2,1)} %x_hbm.3, bf16[5120]{0:T(1024)(128)(2,1)} %gain_hbm.1, ...), custom_call_target="tpu_custom_call" | custom-call | flops 1073741824 | bytes 134217728 | tf_op jit(solution)/shard_map/pallas_call | solution.py:360
  198.7 4.2 %shard_map.140 = (bf16[2,5120]{1,0:T(2,128)(2,1)}, bf16[2,8192,128]{2,1,0:T(8,128)(2,1)}, bf16[2,8192,128]{2,1,0:T(8,128)(2,1)}) custom-call(bf16[16,5120]{1,0:T(8,128)(2,1)S(1)} %get-tuple-element.11.o_ref, bf16[2,8192,128]{2,1,0:T(8,128)(2,1)S(1)} %get-tuple-element.12.k_land, bf16[2,8192,128]{2,1,0:T(8,128)(2,1)S(1)} %get-tuple-element.13.v_land, ...), custom_call_target="tpu_custom_call" | custom-call | flops 1073741824 | bytes 33554432 | tf_op jit(solution)/shard_map/pallas_call | solution.py:401

commit v11 on v10

--- a/solution.py
+++ b/solution.py
@@ -16,6 +16,7 @@
 OUT_TILE = 512
 LHS_ROWS = 16
 CORES = 2
+LAST = 3 * CORES
 MESH = pl.DeviceIdType.MESH
 
 
@@ -100,25 +101,36 @@
     for d in range(1, (chips - 1) // 2 + 1):
         pairs += [(d, 0), (-d, 0), (d, 1), (-d, 1)]
     near = len(pairs)
+    split = near - 2 * CORES
     if chips % 2 == 0:
         pairs += [(chips // 2, 0), (chips // 2, 1)]
-    for c, src, land, peers in ((0, k_ref, k_land, range(near)), (1, v_ref, v_land, range(near)),
+    for c, src, land, peers in ((0, k_ref, k_land, range(near)), (1, v_ref, v_land, range(split)),
                                 (0, k_ref, k_land, range(near, n - 1))):
         for i in peers:
             push(c, src, land, i).start()
     own_copy(0, k_ref, k_land).start()
     own_copy(1, v_ref, v_land).start()
 
-    last = range(n - 1 - near)
+    last = range(n - 1 - split)
+
+    def mirrored(f):
+        offset, flip = pairs[split + f]
+        return pairs.index((-offset, flip)) - split if (-offset, flip) in pairs else f
 
     def stage_copy(f):
-        return pltpu.make_async_copy(v_ref.at[pl.ds(partner(near + f) * rows, rows)], staged.at[f], stage_sem.at[f])
+        return pltpu.make_async_copy(v_ref.at[pl.ds(partner(split + f) * rows, rows)], staged.at[f], stage_sem.at[f])
 
     def push_half(part, f):
         return pltpu.make_async_remote_copy(
-            src_ref=packed.at[part, f], dst_ref=half_land.at[part, f],
+            src_ref=packed.at[part, f], dst_ref=half_land.at[part, mirrored(f)],
+            send_sem=half_send.at[part, f], recv_sem=half_recv.at[part, mirrored(f)],
+            device_id=(group_id, partner(split + f)), device_id_type=MESH)
+
+    def half_arrival(part, f):
+        return pltpu.make_async_remote_copy(
+            src_ref=half_land.at[part, f], dst_ref=half_land.at[part, f],
             send_sem=half_send.at[part, f], recv_sem=half_recv.at[part, f],
-            device_id=(group_id, partner(near + f)), device_id_type=MESH)
+            device_id=(group_id, me), device_id_type=MESH)
 
     for f in last:
         stage_copy(f).start()
@@ -267,9 +279,9 @@
 
     def value_half(part):
         for f in last:
-            push_half(part, f).wait_recv()
+            half_arrival(part, f).wait_recv()
             for s in range(rows):
-                vals, place = settle_half(s, f, partner(near + f), part)
+                vals, place = settle_half(s, f, partner(split + f), part)
                 weigh(s, place, vals, part == 0)
 
     def finish_heads(part):
@@ -296,7 +308,7 @@
         m_acc[s] = jnp.broadcast_to(jnp.max(m_acc[s], axis=-1, keepdims=True), (heads, head_dim))
     own_copy(1, v_ref, v_land).wait()
     value_chunk(me)
-    for i in range(near):
+    for i in range(split):
         source = partner(i)
         arrival(1, v_land, source).wait_recv()
         value_chunk(source)
@@ -314,7 +326,7 @@
     for r in range(depth // block // 2, depth // block):
         wait_weights(14 + r)
     for c, (src, land) in enumerate(((k_ref, k_land), (v_ref, v_land))):
-        for i in range(n - 1 if c == 0 else near):
+        for i in range(n - 1 if c == 0 else split):
             push(c, src, land, i).wait_send()
     for part in range(2):
         for f in last:
@@ -382,19 +394,19 @@
                 pltpu.VMEM((rows, heads, head_dim), f32),
                 pltpu.VMEM((rows, heads, head_dim), f32),
                 pltpu.VMEM((LHS_ROWS, width), f32),
-                pltpu.VMEM((CORES, rows, chunk, head_dim), bf16),
-                pltpu.VMEM((2, CORES, rows, chunk // 2, head_dim), bf16),
-                pltpu.VMEM((2, CORES, rows, chunk // 2, head_dim), bf16),
+                pltpu.VMEM((LAST, rows, chunk, head_dim), bf16),
+                pltpu.VMEM((2, LAST, rows, chunk // 2, head_dim), bf16),
+                pltpu.VMEM((2, LAST, rows, chunk // 2, head_dim), bf16),
                 pltpu.SemaphoreType.DMA((6,)),
                 pltpu.SemaphoreType.DMA((RING, PACK)),
                 pltpu.SemaphoreType.DMA((2,)),
                 pltpu.SemaphoreType.DMA((2, n)),
                 pltpu.SemaphoreType.DMA((2, n)),
-                pltpu.SemaphoreType.DMA((CORES,)),
-                pltpu.SemaphoreType.DMA((2, CORES)),
-                pltpu.SemaphoreType.DMA((2, CORES)),
+                pltpu.SemaphoreType.DMA((LAST,)),
+                pltpu.SemaphoreType.DMA((2, LAST)),
+                pltpu.SemaphoreType.DMA((2, LAST)),
             ],
-            compiler_params=pltpu.CompilerParams(collective_id=0, has_side_effects=True, vmem_limit_bytes=8 * 1024 * 1024),
+            compiler_params=pltpu.CompilerParams(collective_id=0, has_side_effects=True, vmem_limit_bytes=9 * 1024 * 1024),
             cost_estimate=pl.CostEstimate(flops=1 << 30, bytes_accessed=1 << 27, transcendentals=0),
         )(prompt_lens, x_tok, norm_gain, b_q, b_k, b_v,
           k_cache.reshape(batch, chunk, head_dim), v_cache.reshape(batch, chunk, head_dim), w_q, w_k, w_v, w_o)
@@ -408,7 +420,7 @@
                 pltpu.VMEM((LHS_ROWS, depth), f32),
                 pltpu.SemaphoreType.DMA((3,)),
             ],
-            compiler_params=pltpu.CompilerParams(vmem_limit_bytes=8 * 1024 * 1024),
+            compiler_params=pltpu.CompilerParams(vmem_limit_bytes=9 * 1024 * 1024),
             cost_estimate=pl.CostEstimate(flops=1 << 30, bytes_accessed=1 << 25, transcendentals=0),
         )(*[pltpu.with_memory_space_constraint(a, pltpu.VMEM) for a in (o_rows, k_all, v_all, ring, y_part)], x_tok)
         shape = (rows, n * span, kv_heads, head_dim)

time: 203 us -> 203 us (level)
  no operation moved by 1% of the time
where the time goes in v11:
time: 203 us
  Pallas kernels  202 us (100%)
    pallas_call x1, Pallas kernels, per_device(): pl.pallas_call(functools.partial(exchange_kernel, dims), out_shape=(pltpu...  198 us
    pallas_call x1, Pallas kernels, per_device(): pl.pallas_call(functools.partial(output_kernel, 14, depth // block // 2),...  4.16 us

profile of v11, /device:TPU:53, one launch (start us, length us, event | category | flops | bytes accessed | tf_op | source)
XLA Modules:
  0.0 203.0 jit_solution(17043832782824267027)
XLA Ops:
  0.6 198.1 %shard_map.139 = (bf16[16,5120]{1,0:T(8,128)(2,1)S(1)}, bf16[2,8192,128]{2,1,0:T(8,128)(2,1)S(1)}, bf16[2,8192,128]{2,1,0:T(8,128)(2,1)S(1)}, bf16[8,512,5120]{2,1,0:T(8,128)(2,1)S(1)}, f32[16,5120]{1,0:T(8,128)S(1)}) custom-call(s32[32]{0:T(128)} %lens_hbm.1, bf16[2,5120]{1,0:T(2,128)(2,1)} %x_hbm.3, bf16[5120]{0:T(1024)(128)(2,1)} %gain_hbm.1, ...), custom_call_target="tpu_custom_call" | custom-call | flops 1073741824 | bytes 134217728 | tf_op jit(solution)/shard_map/pallas_call | solution.py:372
  198.7 4.2 %shard_map.140 = (bf16[2,5120]{1,0:T(2,128)(2,1)}, bf16[2,8192,128]{2,1,0:T(8,128)(2,1)}, bf16[2,8192,128]{2,1,0:T(8,128)(2,1)}) custom-call(bf16[16,5120]{1,0:T(8,128)(2,1)S(1)} %get-tuple-element.11.o_ref, bf16[2,8192,128]{2,1,0:T(8,128)(2,1)S(1)} %get-tuple-element.12.k_land, bf16[2,8192,128]{2,1,0:T(8,128)(2,1)S(1)} %get-tuple-element.13.v_land, ...), custom_call_target="tpu_custom_call" | custom-call | flops 1073741824 | bytes 33554432 | tf_op jit(solution)/shard_map/pallas_call | solution.py:413

commit v12 on v10

--- a/solution.py
+++ b/solution.py
@@ -102,8 +102,7 @@
     near = len(pairs)
     if chips % 2 == 0:
         pairs += [(chips // 2, 0), (chips // 2, 1)]
-    for c, src, land, peers in ((0, k_ref, k_land, range(near)), (1, v_ref, v_land, range(near)),
-                                (0, k_ref, k_land, range(near, n - 1))):
+    for c, src, land, peers in ((0, k_ref, k_land, range(n - 1)), (1, v_ref, v_land, range(near))):
         for i in peers:
             push(c, src, land, i).start()
     own_copy(0, k_ref, k_land).start()

time: 203 us -> 204 us (level)
  no operation moved by 1% of the time
where the time goes in v12:
time: 204 us; the launch traced here: 203 us
  Pallas kernels  203 us (100%)
    pallas_call x1, Pallas kernels, per_device(): pl.pallas_call(functools.partial(exchange_kernel, dims), out_shape=(pltpu...  198 us
    pallas_call x1, Pallas kernels, per_device(): pl.pallas_call(functools.partial(output_kernel, 14, depth // block // 2),...  4.16 us

profile of v12, /device:TPU:53, one launch (start us, length us, event | category | flops | bytes accessed | tf_op | source)
XLA Modules:
  0.0 203.4 jit_solution(7397022562507407409)
XLA Ops:
  0.6 198.5 %shard_map.139 = (bf16[16,5120]{1,0:T(8,128)(2,1)S(1)}, bf16[2,8192,128]{2,1,0:T(8,128)(2,1)S(1)}, bf16[2,8192,128]{2,1,0:T(8,128)(2,1)S(1)}, bf16[8,512,5120]{2,1,0:T(8,128)(2,1)S(1)}, f32[16,5120]{1,0:T(8,128)S(1)}) custom-call(s32[32]{0:T(128)} %lens_hbm.1, bf16[2,5120]{1,0:T(2,128)(2,1)} %x_hbm.3, bf16[5120]{0:T(1024)(128)(2,1)} %gain_hbm.1, ...), custom_call_target="tpu_custom_call" | custom-call | flops 1073741824 | bytes 134217728 | tf_op jit(solution)/shard_map/pallas_call | solution.py:359
  199.1 4.2 %shard_map.140 = (bf16[2,5120]{1,0:T(2,128)(2,1)}, bf16[2,8192,128]{2,1,0:T(8,128)(2,1)}, bf16[2,8192,128]{2,1,0:T(8,128)(2,1)}) custom-call(bf16[16,5120]{1,0:T(8,128)(2,1)S(1)} %get-tuple-element.11.o_ref, bf16[2,8192,128]{2,1,0:T(8,128)(2,1)S(1)} %get-tuple-element.12.k_land, bf16[2,8192,128]{2,1,0:T(8,128)(2,1)S(1)} %get-tuple-element.13.v_land, ...), custom_call_target="tpu_custom_call" | custom-call | flops 1073741824 | bytes 33554432 | tf_op jit(solution)/shard_map/pallas_call | solution.py:400

commit v13 on v12

--- a/solution.py
+++ b/solution.py
@@ -100,9 +100,10 @@
     for d in range(1, (chips - 1) // 2 + 1):
         pairs += [(d, 0), (-d, 0), (d, 1), (-d, 1)]
     near = len(pairs)
+    split = near - 2 * CORES
     if chips % 2 == 0:
         pairs += [(chips // 2, 0), (chips // 2, 1)]
-    for c, src, land, peers in ((0, k_ref, k_land, range(n - 1)), (1, v_ref, v_land, range(near))):
+    for c, src, land, peers in ((0, k_ref, k_land, range(n - 1)), (1, v_ref, v_land, range(split))):
         for i in peers:
             push(c, src, land, i).start()
     own_copy(0, k_ref, k_land).start()
@@ -178,9 +179,12 @@
         if b + RING < 14 + RING:
             start_weights(b + RING)
 
-    for part in range(2):
-        for f in last:
-            push_half(part, f).start()
+    for f in last:
+        push_half(0, f).start()
+    for i in range(split, near):
+        push(1, v_ref, v_land, i).start()
+    for f in last:
+        push_half(1, f).start()
 
     lane = lax.broadcasted_iota(jnp.int32, (1, head_dim), 1)
     freq_idx = jnp.where(lane < half_dim, lane, lane - half_dim).astype(jnp.float32)

time: 204 us -> 198 us (0.971)
  Pallas kernels: 203 us -> 198 us
    pallas_call x1, Pallas kernels: 198 us -> 194 us  [per_device(): pl.pallas_call(functools.partial(exchange_kernel, dims), out_shape=(pltpu...]
where the time goes in v13:
time: 198 us
  Pallas kernels  198 us (100%)
    pallas_call x1, Pallas kernels, per_device(): pl.pallas_call(functools.partial(exchange_kernel, dims), out_shape=(pltpu...  194 us
    pallas_call x1, Pallas kernels, per_device(): pl.pallas_call(functools.partial(output_kernel, 14, depth // block // 2),...  4.16 us

profile of v13, /device:TPU:53, one launch (start us, length us, event | category | flops | bytes accessed | tf_op | source)
XLA Modules:
  0.0 198.4 jit_solution(2919285988574909571)
XLA Ops:
  0.6 193.6 %shard_map.139 = (bf16[16,5120]{1,0:T(8,128)(2,1)S(1)}, bf16[2,8192,128]{2,1,0:T(8,128)(2,1)S(1)}, bf16[2,8192,128]{2,1,0:T(8,128)(2,1)S(1)}, bf16[8,512,5120]{2,1,0:T(8,128)(2,1)S(1)}, f32[16,5120]{1,0:T(8,128)S(1)}) custom-call(s32[32]{0:T(128)} %lens_hbm.1, bf16[2,5120]{1,0:T(2,128)(2,1)} %x_hbm.3, bf16[5120]{0:T(1024)(128)(2,1)} %gain_hbm.1, ...), custom_call_target="tpu_custom_call" | custom-call | flops 1073741824 | bytes 134217728 | tf_op jit(solution)/shard_map/pallas_call | solution.py:363
  194.2 4.2 %shard_map.140 = (bf16[2,5120]{1,0:T(2,128)(2,1)}, bf16[2,8192,128]{2,1,0:T(8,128)(2,1)}, bf16[2,8192,128]{2,1,0:T(8,128)(2,1)}) custom-call(bf16[16,5120]{1,0:T(8,128)(2,1)S(1)} %get-tuple-element.11.o_ref, bf16[2,8192,128]{2,1,0:T(8,128)(2,1)S(1)} %get-tuple-element.12.k_land, bf16[2,8192,128]{2,1,0:T(8,128)(2,1)S(1)} %get-tuple-element.13.v_land, ...), custom_call_target="tpu_custom_call" | custom-call | flops 1073741824 | bytes 33554432 | tf_op jit(solution)/shard_map/pallas_call | solution.py:404

commit v14 on v13

--- a/solution.py
+++ b/solution.py
@@ -103,7 +103,8 @@
     split = near - 2 * CORES
     if chips % 2 == 0:
         pairs += [(chips // 2, 0), (chips // 2, 1)]
-    for c, src, land, peers in ((0, k_ref, k_land, range(n - 1)), (1, v_ref, v_land, range(split))):
+    for c, src, land, peers in ((0, k_ref, k_land, range(near)), (1, v_ref, v_land, range(split)),
+                                (0, k_ref, k_land, range(near, n - 1))):
         for i in peers:
             push(c, src, land, i).start()
     own_copy(0, k_ref, k_land).start()

time: 198 us -> 200 us (1.010)
  no operation moved by 1% of the time
where the time goes in v14:
time: 200 us
  Pallas kernels  199 us (100%)
    pallas_call x1, Pallas kernels, per_device(): pl.pallas_call(functools.partial(exchange_kernel, dims), out_shape=(pltpu...  195 us
    pallas_call x1, Pallas kernels, per_device(): pl.pallas_call(functools.partial(output_kernel, 14, depth // block // 2),...  4.16 us

profile of v14, /device:TPU:53, one launch (start us, length us, event | category | flops | bytes accessed | tf_op | source)
XLA Modules:
  0.0 199.8 jit_solution(8755763001903512280)
XLA Ops:
  0.6 195.0 %shard_map.139 = (bf16[16,5120]{1,0:T(8,128)(2,1)S(1)}, bf16[2,8192,128]{2,1,0:T(8,128)(2,1)S(1)}, bf16[2,8192,128]{2,1,0:T(8,128)(2,1)S(1)}, bf16[8,512,5120]{2,1,0:T(8,128)(2,1)S(1)}, f32[16,5120]{1,0:T(8,128)S(1)}) custom-call(s32[32]{0:T(128)} %lens_hbm.1, bf16[2,5120]{1,0:T(2,128)(2,1)} %x_hbm.3, bf16[5120]{0:T(1024)(128)(2,1)} %gain_hbm.1, ...), custom_call_target="tpu_custom_call" | custom-call | flops 1073741824 | bytes 134217728 | tf_op jit(solution)/shard_map/pallas_call | solution.py:364
  195.7 4.2 %shard_map.140 = (bf16[2,5120]{1,0:T(2,128)(2,1)}, bf16[2,8192,128]{2,1,0:T(8,128)(2,1)}, bf16[2,8192,128]{2,1,0:T(8,128)(2,1)}) custom-call(bf16[16,5120]{1,0:T(8,128)(2,1)S(1)} %get-tuple-element.11.o_ref, bf16[2,8192,128]{2,1,0:T(8,128)(2,1)S(1)} %get-tuple-element.12.k_land, bf16[2,8192,128]{2,1,0:T(8,128)(2,1)S(1)} %get-tuple-element.13.v_land, ...), custom_call_target="tpu_custom_call" | custom-call | flops 1073741824 | bytes 33554432 | tf_op jit(solution)/shard_map/pallas_call | solution.py:405
